TPU v7x, 512 devices: a whole 4x4x16 slice. The times are simulated.
512 devices in a mesh: row: 64 (over z, x), col: 8 (over y, core).
Axes of the slice: x: 4, y: 4, z: 16, core: 2. Of those that a mesh axis runs over, the one named last changes fastest.
Arguments:
- gate_up: bfloat16 [4, 2, 14336, 4096], P(None, None, 'row', 'col'), may hold values from -0.09375 to 0.09375
- down_weight: bfloat16 [4, 4096, 14336], P(None, 'row', 'col'), may hold values from -0.046875 to 0.046875
- query_output: bfloat16 [4, 2, 4096, 4096], P(None, None, 'row', 'col'), may hold values from -0.09375 to 0.09375
- probe_gate: bfloat16 [4, 2, 16, 4096], P(None, None, None, 'col'), may hold values from -6 to 6
- probe_down: bfloat16 [4, 16, 14336], P(None, None, 'col'), may hold values from -6 to 6
- probe_query: bfloat16 [4, 2, 16, 4096], P(None, None, None, 'col'), may hold values from -6 to 6
Outputs:
- vector_gate: float32 [4, 2, 16, 4096], P(None, None, None, 'col')
- vector_down: float32 [4, 16, 14336], P(None, None, 'col')
- vector_query: float32 [4, 2, 16, 4096], P(None, None, None, 'col')
- sigma_gate: float32 [4, 2, 16], replicated
- sigma_down: float32 [4, 16], replicated
- sigma_query: float32 [4, 2, 16], replicated
All inputs are finite; a program needn't handle non-finite values.
Results may differ from a plain program's by a relative error of at most 0.0033.
Values may be sent and summed in bfloat16 or wider, within the bound.
No kernel may reach another device: no remote copies, remote signals or barrier semaphores. Data moves between devices by JAX's collectives and lax.ppermute only.
A program may use at most 64 MiB of HBM per device.

v0:
```python
import jax
import jax.numpy as jnp
from jax import lax
from jax.sharding import Mesh
from jax.sharding import PartitionSpec as P

ITERS = 2
ROW = ("row_0", "row_1")


epsilon = 1e-06


def copy_for_each(shard, axis):
    length = lax.axis_size(axis)
    return lax.all_to_all(
        jnp.broadcast_to(shard[None], (length, *shard.shape)), axis, 0, 0, tiled=True
    )


def of_everyone(shard, axis):
    everything = copy_for_each(shard, axis)
    return jnp.sum(everything, axis=0)


def over_axes(shard, axes):
    for axis in axes:
        shard = lax.psum(shard, axis)
    return shard


def body(gate_up, down_weight, query_output, probe_gate, probe_down, probe_query):
    row_count = lax.axis_size(ROW)
    col_count = lax.axis_size("col")
    weights = (gate_up, down_weight[:, None], query_output)
    vectors = (probe_gate, probe_down[:, None], probe_query)
    scaled_right = vectors
    spectral = None

    def left_factor(total, weight):
        return lax.rsqrt(total[..., None] / (weight.shape[2] * row_count) + epsilon)

    for turn in range(ITERS):
        partial_value = tuple(
            (
                jnp.einsum("lmoi,lmki->lmko", weight, vector, preferred_element_type=jnp.float32)
                for weight, vector in zip(weights, vectors)
            )
        )
        summed = jax.tree.map(lambda part: of_everyone(part, "col"), partial_value)
        squares = tuple((jnp.sum(piece * piece, axis=3) for piece in summed))
        totals = jax.tree.map(lambda part: over_axes(part, ROW), squares)
        left_vecs = tuple((piece.astype(jnp.bfloat16) for piece in summed))
        right_partial = tuple(
            (
                jnp.einsum("lmoi,lmko->lmki", weight, left, preferred_element_type=jnp.float32)
                for weight, left in zip(weights, left_vecs)
            )
        )
        raw_sums = lax.psum(right_partial, ROW)
        right_sums = tuple(
            (
                raw * left_factor(total, weight)
                for raw, total, weight in zip(raw_sums, totals, weights)
            )
        )
        right_squares = tuple((jnp.sum(piece * piece, axis=3) for piece in right_sums))
        right_totals = jax.tree.map(lambda part: of_everyone(part, "col"), right_squares)
        scaled_right = tuple(
            (
                piece * lax.rsqrt(total[..., None] / (piece.shape[3] * col_count) + epsilon)
                for piece, total in zip(right_sums, right_totals)
            )
        )
        spectral = tuple(
            (
                jnp.sqrt(total / (weight.shape[2] * row_count))
                for weight, total in zip(weights, right_totals)
            )
        )
        vectors = tuple((piece.astype(jnp.bfloat16) for piece in scaled_right))
    return (
        scaled_right[0],
        scaled_right[1][:, 0],
        scaled_right[2],
        spectral[0],
        spectral[1][:, 0],
        spectral[2],
    )


def solution(mesh):
    finer = Mesh(mesh.devices.reshape(16, 4, mesh.shape["col"]), ("row_0", "row_1", "col"))
    in_specs = (
        P(None, None, ROW, "col"),
        P(None, ROW, "col"),
        P(None, None, ROW, "col"),
        P(None, None, None, "col"),
        P(None, None, "col"),
        P(None, None, None, "col"),
    )
    out_specs = (
        P(None, None, None, "col"),
        P(None, None, "col"),
        P(None, None, None, "col"),
        P(),
        P(),
        P(),
    )
    return jax.shard_map(body, mesh=finer, in_specs=in_specs, out_specs=out_specs, check_vma=False)
```

profile of v0, /device:TPU:1, one launch (start us, length us, event | category | flops | bytes accessed | tf_op | source)
XLA Modules:
  0.0 717.1 jit_solution(13803138326627123436)
XLA Ops:
  9.9 10.1 %all-to-all-start.4 = ((f32[8,1,4096]{2,1,0:T(1,128)}), f32[8,1,4096]{2,1,0:T(1,128)S(1)}, u32[]{:S(2)}, u32[]{:S(2)}) async-start(f32[8,1,4096]{2,1,0:T(1,128)} %reshape.197), calls=%async_computation.4 | async-start | bytes 262144 | tf_op jit(solution)/shard_map/all_to_all | solution.py:16
  21.3 3.9 all-to-all-done.4
  25.2 4.2 all-to-all-start.8
  30.7 5.2 all-to-all-done.8
  38.1 5.1 all-to-all-start
  43.7 2.4 reduce.10
  61.1 45.7 %all-reduce.3 = (f32[4,2,16]{2,1,0:T(2,128)S(1)}, f32[4,1,16]{2,0,1:T(4,128)S(1)}, f32[4,2,16]{2,1,0:T(2,128)S(1)}) all-reduce(f32[4,2,16]{2,1,0:T(2,128)S(1)} %multiply_reduce_fusion.7, f32[4,1,16]{2,0,1:T(4,128)S(1)} %bitcast.30, f32[4,2,16]{2,1,0:T(2,128)S(1)} %multiply_reduce_fusion.9), channel_id=1, replica_groups=mesh['row_0'=16,'row_1'=4,'col'=8] {'row_0'}, use_global_device_ids=true, to_apply=%region_3.0 | all-reduce | flops 320 | bytes 2560 | tf_op jit(solution)/shard_map/psum | solution.py:28
  106.7 13.6 %all-reduce.5 = (f32[4,2,16]{2,1,0:T(2,128)S(1)}, f32[4,1,16]{2,0,1:T(4,128)S(1)}, f32[4,2,16]{2,1,0:T(2,128)S(1)}) all-reduce(f32[4,2,16]{2,1,0:T(2,128)S(1)} %get-tuple-element.15, f32[4,1,16]{2,0,1:T(4,128)S(1)} %get-tuple-element.16, f32[4,2,16]{2,1,0:T(2,128)S(1)} %get-tuple-element.17), channel_id=1, replica_groups=mesh['row_0'=16,'row_1'=4,'col'=8] {'row_1'}, use_global_device_ids=true, to_apply=%region_4.0 | all-reduce | flops 320 | bytes 2560 | tf_op jit(solution)/shard_map/psum | solution.py:28
  120.3 203.2 %all-reduce.11.cloned.1.call-done = (f32[4,2,16,512]{3,2,1,0:T(8,128)}, f32[4,1,16,1792]{3,2,0,1:T(8,128)}, f32[4,2,16,512]{3,2,1,0:T(8,128)}) async-done(((f32[4,2,16,512]{3,2,1,0:T(8,128)}, f32[4,1,16,1792]{3,2,0,1:T(8,128)}, f32[4,2,16,512]{3,2,1,0:T(8,128)}), (f32[4,2,16,512]{3,2,1,0:T(8,128)}, f32[4,1,16,1792]{3,2,0,1:T(8,128)}, f32[4,2,16,512]{3,2,1,0:T(8,128)})) %all-reduce.11.cloned.1.call-update) | async-done | bytes 983056 | tf_op jit(solution)/shard_map/psum | solution.py:60
  325.4 15.1 %all-to-all-start.5 = ((f32[8,4,1,16]{3,2,1,0:T(1,128)}), f32[8,4,1,16]{3,2,1,0:T(1,128)S(1)}, u32[]{:S(2)}, u32[]{:S(2)}) async-start(f32[8,4,1,16]{3,2,1,0:T(1,128)} %broadcast_in_dim.29), calls=%async_computation.5 | async-start | bytes 32768 | tf_op jit(solution)/shard_map/all_to_all | solution.py:16
  345.1 3.9 all-to-all-start.9
  354.2 4.3 all-to-all-start.1
  365.5 4.8 all-to-all-start.6
  372.4 3.3 all-to-all-done.6
  375.6 4.8 all-to-all-start.10
  381.7 5.3 all-to-all-done.10
  389.1 5.1 all-to-all-start.2
  403.4 6.0 all-to-all-done.2
  412.1 41.4 %all-reduce.2 = (f32[4,2,16]{2,1,0:T(2,128)S(1)}, f32[4,1,16]{2,0,1:T(4,128)S(1)}, f32[4,2,16]{2,1,0:T(2,128)S(1)}) all-reduce(f32[4,2,16]{2,1,0:T(2,128)S(1)} %multiply_reduce_fusion.6, f32[4,1,16]{2,0,1:T(4,128)S(1)} %bitcast.31, f32[4,2,16]{2,1,0:T(2,128)S(1)} %multiply_reduce_fusion.8), channel_id=1, replica_groups=mesh['row_0'=16,'row_1'=4,'col'=8] {'row_0'}, use_global_device_ids=true, to_apply=%region_10.0 | all-reduce | flops 320 | bytes 2560 | tf_op jit(solution)/shard_map/psum | solution.py:28
  453.4 13.0 %all-reduce.4 = (f32[4,2,16]{2,1,0:T(2,128)S(1)}, f32[4,1,16]{2,0,1:T(4,128)S(1)}, f32[4,2,16]{2,1,0:T(2,128)S(1)}) all-reduce(f32[4,2,16]{2,1,0:T(2,128)S(1)} %get-tuple-element.12, f32[4,1,16]{2,0,1:T(4,128)S(1)} %get-tuple-element.13, f32[4,2,16]{2,1,0:T(2,128)S(1)} %get-tuple-element.14), channel_id=1, replica_groups=mesh['row_0'=16,'row_1'=4,'col'=8] {'row_1'}, use_global_device_ids=true, to_apply=%region_11.0 | all-reduce | flops 320 | bytes 2560 | tf_op jit(solution)/shard_map/psum | solution.py:28
  466.4 203.1 %all-reduce.9.cloned.1.call-done = (f32[4,2,16,512]{3,2,1,0:T(8,128)}, f32[4,1,16,1792]{3,2,0,1:T(8,128)}, f32[4,2,16,512]{3,2,1,0:T(8,128)}) async-done(((f32[4,2,16,512]{3,2,1,0:T(8,128)}, f32[4,1,16,1792]{3,2,0,1:T(8,128)}, f32[4,2,16,512]{3,2,1,0:T(8,128)}), (f32[4,2,16,512]{3,2,1,0:T(8,128)}, f32[4,1,16,1792]{3,2,0,1:T(8,128)}, f32[4,2,16,512]{3,2,1,0:T(8,128)})) %all-reduce.9.cloned.1.call-update) | async-done | bytes 983056 | tf_op jit(solution)/shard_map/psum | solution.py:60
  671.5 15.1 %all-to-all-start.7 = ((f32[8,4,1,16]{3,2,1,0:T(1,128)}), f32[8,4,1,16]{3,2,1,0:T(1,128)S(1)}, u32[]{:S(2)}, u32[]{:S(2)}) async-start(f32[8,4,1,16]{3,2,1,0:T(1,128)} %broadcast_in_dim.31), calls=%async_computation.7 | async-start | bytes 32768 | tf_op jit(solution)/shard_map/all_to_all | solution.py:16
  691.2 3.9 all-to-all-start.11
  699.7 3.9 all-to-all-start.3
  (123 shorter events, 76.3 us)
Async XLA Ops:
  7.2 22.3 %copy-start = (bf16[4,2,224,512]{3,2,1,0:T(8,128)(2,1)S(1)}, bf16[4,2,224,512]{3,2,1,0:T(8,128)(2,1)}, u32[]{:S(2)}) copy-start(bf16[4,2,224,512]{3,2,1,0:T(8,128)(2,1)} %param.6) | copy-start | bytes 5505028
  7.2 12.8 %copy-start.11 = (bf16[4,2,16,512]{3,2,1,0:T(8,128)(2,1)S(1)}, bf16[4,2,16,512]{3,2,1,0:T(8,128)(2,1)}, u32[]{:S(2)}) copy-start(bf16[4,2,16,512]{3,2,1,0:T(8,128)(2,1)} %param.11) | copy-start | bytes 393220
  7.2 12.8 %copy-start.2 = (bf16[4,2,64,512]{3,2,1,0:T(8,128)(2,1)S(1)}, bf16[4,2,64,512]{3,2,1,0:T(8,128)(2,1)}, u32[]{:S(2)}) copy-start(bf16[4,2,64,512]{3,2,1,0:T(8,128)(2,1)} %param.8) | copy-start | bytes 1572868
  9.0 20.4 %copy-start.10 = (bf16[4,2,16,512]{3,2,1,0:T(8,128)(2,1)S(1)}, bf16[4,2,16,512]{3,2,1,0:T(8,128)(2,1)}, u32[]{:S(2)}) copy-start(bf16[4,2,16,512]{3,2,1,0:T(8,128)(2,1)} %param.9) | copy-start | bytes 393220
  9.9 15.4 %all-to-all-start.4 = ((f32[8,1,4096]{2,1,0:T(1,128)}), f32[8,1,4096]{2,1,0:T(1,128)S(1)}, u32[]{:S(2)}, u32[]{:S(2)}) async-start(f32[8,1,4096]{2,1,0:T(1,128)} %reshape.197), calls=%async_computation.4 | async-start | bytes 262144 | tf_op jit(solution)/shard_map/all_to_all | solution.py:16
  25.2 4.2 copy-start.7
  25.2 10.7 %all-to-all-start.8 = ((f32[8,1,8192]{2,1,0:T(1,128)}), f32[8,1,8192]{2,1,0:T(1,128)S(1)}, u32[]{:S(2)}, u32[]{:S(2)}) async-start(f32[8,1,8192]{2,1,0:T(1,128)} %reshape.201), calls=%async_computation.8 | async-start | bytes 524288 | tf_op jit(solution)/shard_map/all_to_all | solution.py:16
  30.7 18.8 %copy-start.1 = (bf16[4,64,1792]{2,1,0:T(8,128)(2,1)S(1)}, bf16[4,64,1792]{2,1,0:T(8,128)(2,1)}, u32[]{:S(2)}) copy-start(bf16[4,64,1792]{2,1,0:T(8,128)(2,1)} %param.7) | copy-start | bytes 2752516
  35.9 12.0 %copy-start.4 = (f32[8,1,8192]{2,1,0:T(1,128)}, f32[8,1,8192]{2,1,0:T(1,128)S(1)}, u32[]{:S(2)}) copy-start(f32[8,1,8192]{2,1,0:T(1,128)S(1)} %all-to-all-done.8) | copy-start | bytes 786436
  38.1 20.2 %all-to-all-start = ((f32[8,4,2,16,224]{4,3,2,1,0:T(8,128)}), f32[8,4,2,16,224]{4,3,2,1,0:T(8,128)}, u32[]{:S(2)}, u32[]{:S(2)}) async-start(f32[8,4,2,16,224]{4,3,2,1,0:T(8,128)} %broadcast_in_dim.24), calls=%async_computation | async-start | bytes 2097152 | tf_op jit(solution)/shard_map/all_to_all | solution.py:16
  43.2 280.4 %all-reduce.11.cloned.1.call-start = ((), (), s32[]{:S(2)}) async-start(), calls=%async_computation.13 | async-start | bytes 1966080 | tf_op jit(solution)/shard_map/psum | solution.py:60
  325.4 19.7 %all-to-all-start.5 = ((f32[8,4,1,16]{3,2,1,0:T(1,128)}), f32[8,4,1,16]{3,2,1,0:T(1,128)S(1)}, u32[]{:S(2)}, u32[]{:S(2)}) async-start(f32[8,4,1,16]{3,2,1,0:T(1,128)} %broadcast_in_dim.29), calls=%async_computation.5 | async-start | bytes 32768 | tf_op jit(solution)/shard_map/all_to_all | solution.py:16
  345.1 8.5 %all-to-all-start.9 = ((f32[8,1,128]{2,1,0:T(1,128)}), f32[8,1,128]{2,1,0:T(1,128)S(1)}, u32[]{:S(2)}, u32[]{:S(2)}) async-start(f32[8,1,128]{2,1,0:T(1,128)} %reshape.203), calls=%async_computation.9 | async-start | bytes 8192 | tf_op jit(solution)/shard_map/all_to_all | solution.py:16
  351.3 29.1 %copy-start.3 = (f32[4,2,16,512]{3,2,1,0:T(8,128)S(1)}, f32[4,2,16,512]{3,2,1,0:T(8,128)}, u32[]{:S(2)}) copy-start(f32[4,2,16,512]{3,2,1,0:T(8,128)} %get-tuple-element.9) | copy-start | bytes 786436
  354.2 11.3 %all-to-all-start.1 = ((f32[8,1,128]{2,1,0:T(1,128)}), f32[8,1,128]{2,1,0:T(1,128)S(1)}, u32[]{:S(2)}, u32[]{:S(2)}) async-start(f32[8,1,128]{2,1,0:T(1,128)} %reshape.193), calls=%async_computation.1 | async-start | bytes 8192 | tf_op jit(solution)/shard_map/all_to_all | solution.py:16
  365.5 10.2 %all-to-all-start.6 = ((f32[8,1,4096]{2,1,0:T(1,128)}), f32[8,1,4096]{2,1,0:T(1,128)}, u32[]{:S(2)}, u32[]{:S(2)}) async-start(f32[8,1,4096]{2,1,0:T(1,128)} %reshape.199), calls=%async_computation.6 | async-start | bytes 262144 | tf_op jit(solution)/shard_map/all_to_all | solution.py:16
  375.6 11.4 %all-to-all-start.10 = ((f32[8,1,8192]{2,1,0:T(1,128)}), f32[8,1,8192]{2,1,0:T(1,128)}, u32[]{:S(2)}, u32[]{:S(2)}) async-start(f32[8,1,8192]{2,1,0:T(1,128)} %reshape.205), calls=%async_computation.10 | async-start | bytes 524288 | tf_op jit(solution)/shard_map/all_to_all | solution.py:16
  389.1 20.2 %all-to-all-start.2 = ((f32[8,4,2,16,224]{4,3,2,1,0:T(8,128)}), f32[8,4,2,16,224]{4,3,2,1,0:T(8,128)}, u32[]{:S(2)}, u32[]{:S(2)}) async-start(f32[8,4,2,16,224]{4,3,2,1,0:T(8,128)} %broadcast_in_dim.26), calls=%async_computation.2 | async-start | bytes 2097152 | tf_op jit(solution)/shard_map/all_to_all | solution.py:16
  394.2 275.3 %all-reduce.9.cloned.1.call-start = ((), (), s32[]{:S(2)}) async-start(), calls=%async_computation.12 | async-start | bytes 1966080 | tf_op jit(solution)/shard_map/psum | solution.py:60
  669.6 35.3 %copy-start.6 = (f32[4,2,16,512]{3,2,1,0:T(8,128)S(1)}, f32[4,2,16,512]{3,2,1,0:T(8,128)}, u32[]{:S(2)}) copy-start(f32[4,2,16,512]{3,2,1,0:T(8,128)} %get-tuple-element.8) | copy-start | bytes 786436
  669.6 39.9 %copy-start.5 = (f32[4,2,16,512]{3,2,1,0:T(8,128)S(1)}, f32[4,2,16,512]{3,2,1,0:T(8,128)}, u32[]{:S(2)}) copy-start(f32[4,2,16,512]{3,2,1,0:T(8,128)} %get-tuple-element.6) | copy-start | bytes 786436
  671.5 19.7 %all-to-all-start.7 = ((f32[8,4,1,16]{3,2,1,0:T(1,128)}), f32[8,4,1,16]{3,2,1,0:T(1,128)S(1)}, u32[]{:S(2)}, u32[]{:S(2)}) async-start(f32[8,4,1,16]{3,2,1,0:T(1,128)} %broadcast_in_dim.31), calls=%async_computation.7 | async-start | bytes 32768 | tf_op jit(solution)/shard_map/all_to_all | solution.py:16
  691.2 8.5 %all-to-all-start.11 = ((f32[8,1,128]{2,1,0:T(1,128)}), f32[8,1,128]{2,1,0:T(1,128)S(1)}, u32[]{:S(2)}, u32[]{:S(2)}) async-start(f32[8,1,128]{2,1,0:T(1,128)} %reshape.207), calls=%async_computation.11 | async-start | bytes 8192 | tf_op jit(solution)/shard_map/all_to_all | solution.py:16
  699.7 8.5 %all-to-all-start.3 = ((f32[8,1,128]{2,1,0:T(1,128)}), f32[8,1,128]{2,1,0:T(1,128)S(1)}, u32[]{:S(2)}, u32[]{:S(2)}) async-start(f32[8,1,128]{2,1,0:T(1,128)} %reshape.195), calls=%async_computation.3 | async-start | bytes 8192 | tf_op jit(solution)/shard_map/all_to_all | solution.py:16
  (3 other events, 2.8 us)
Sparse Core Ops, SparseCore 0:
  60.9 262.6 all-reduce.10
  411.9 257.6 all-reduce.8
where the time goes:
time: 719 us; the launch traced here: 717 us
  waiting for transfers between devices  439 us (61%)
  blocking collectives  114 us (16%)
  starting transfers between devices  80.4 us (11%)
  other arithmetic  32.7 us (5%)
  local copies, waits for them, and re-layouts  22.5 us (3%)
  matrix products  14.6 us (2%)
  between operations  14.3 us (2%)
    psum x2, waiting for transfers between devices, body(): raw_sums = lax.psum(right_partial, ROW)  406 us
    psum x4, blocking collectives, over_axes(): shard = lax.psum(shard, axis)  114 us
    all_to_all x12, starting transfers between devices, copy_for_each(): lax.all_to_all(jnp.broadcast_to(shard[None], (length, *shard.shape)), axi...  80.4 us
    all_to_all x12, waiting for transfers between devices, copy_for_each(): lax.all_to_all(jnp.broadcast_to(shard[None], (length, *shard.shape)), axi...  32.5 us
    unnamed x42, local copies, waits for them, and re-layouts  14.8 us
  transfers between devices with their start and end apart: 14, of which 13 were waited for; matrix products, arithmetic and copies ran while one was open for 7% of the time, Pallas kernels for 0%

commit v1 on v0

v1 whole, which is shorter than its diff:
```python
import functools

import jax
import jax.numpy as jnp
from jax import lax
from jax.experimental import pallas as pl
from jax.experimental.pallas import tpu as pltpu
from jax.sharding import Mesh
from jax.sharding import PartitionSpec as P

F32 = jnp.float32
BF16 = jnp.bfloat16
EPS = 1e-06
VMEM = pl.BlockSpec(memory_space=pltpu.VMEM)
LANES = 128


def call(kernel, outs, *args):
    return pl.pallas_call(
        kernel,
        out_shape=outs,
        in_specs=[VMEM] * len(args),
        out_specs=jax.tree.map(lambda _: VMEM, outs),
    )(*args)


def sds(shape, dtype):
    return jax.ShapeDtypeStruct(shape, dtype)


class Plan:
    def __init__(self, weights, xs, zs, cols):
        self.xs, self.zs, self.cols = xs, zs, cols
        self.rows = xs * zs
        self.outs = []
        self.ins = []
        self.where = []
        used = [0] * xs
        for w in weights:
            count, out, inp = w.shape
            per = count // xs
            for m in range(count):
                part = m // per
                self.where.append((part, used[part]))
                used[part] += inp // LANES
                self.outs.append(out)
                self.ins.append(inp)
        self.data = max(used)
        self.blocks = -(-(self.data + 2) // zs) * zs
        self.mine = self.blocks // zs
        self.left = []
        at = 0
        for out in self.outs:
            self.left.append(at)
            at += out
        self.left_end = at
        self.left_pad = -(-at // LANES) * LANES
        self.left_width = self.left_pad + LANES


def weight_of(refs, m):
    for ref in refs:
        if m < ref.shape[0]:
            return ref[m]
        m -= ref.shape[0]


def lane_table(columns, probes):
    lane = lax.broadcasted_iota(jnp.int32, (probes, LANES), 1)
    table = jnp.zeros((probes, LANES), F32)
    for m, column in enumerate(columns):
        table = jnp.where(lane == m, column, table)
    return table


def put_left(plan, lefts, table, out_ref):
    whole = jnp.concatenate(lefts, axis=1)
    pad = plan.left_pad - plan.left_end
    if pad:
        whole = jnp.concatenate([whole, jnp.zeros((whole.shape[0], pad), F32)], axis=1)
    for j in range(plan.cols):
        out_ref[j, :, : plan.left_pad] = whole
        out_ref[j, :, plan.left_pad :] = table


def dot_left(v, w):
    return lax.dot_general(v, w, (((1,), (1,)), ((), ())), preferred_element_type=F32)


def first_left(plan, a, b, c, va, vb, vc, out_ref):
    weights, probes = (a, b, c), (va, vb, vc)
    lefts = []
    for m in range(len(plan.outs)):
        lefts.append(dot_left(weight_of(probes, m), weight_of(weights, m)))
    put_left(plan, lefts, jnp.zeros((lefts[0].shape[0], LANES), F32), out_ref)


def vector_of(plan, v_ref, m, probes):
    part, first = plan.where[m]
    n = plan.ins[m] // LANES
    return jnp.concatenate(
        [v_ref[part, (first + k) * probes : (first + k + 1) * probes, :] for k in range(n)], axis=1
    )


def next_left(plan, a, b, c, v_ref, out_ref):
    weights = (a, b, c)
    probes = v_ref.shape[1] // plan.blocks
    lefts, squares = [], []
    for m in range(len(plan.outs)):
        v = vector_of(plan, v_ref, m, probes)
        wide = v.astype(F32)
        squares.append(jnp.sum(wide * wide, axis=1, keepdims=True))
        lefts.append(dot_left(v, weight_of(weights, m)))
    put_left(plan, lefts, lane_table(squares, probes), out_ref)


def right_body(plan, a, b, c, l_ref, out_ref):
    weights = (a, b, c)
    total = l_ref[0]
    for j in range(1, plan.cols):
        total = total + l_ref[j]
    probes = total.shape[0]
    squares = []
    for m in range(len(plan.outs)):
        raw = total[:, plan.left[m] : plan.left[m] + plan.outs[m]]
        squares.append(jnp.sum(raw * raw, axis=1, keepdims=True))
        right = jnp.dot(raw.astype(BF16), weight_of(weights, m), preferred_element_type=F32)
        part, first = plan.where[m]
        for k in range(plan.ins[m] // LANES):
            at = (first + k) * probes
            out_ref[part, at : at + probes, :] = right[:, k * LANES : (k + 1) * LANES]
    table = lane_table(squares, probes)
    zero = jnp.zeros((probes, LANES), F32)
    for x in range(plan.xs):
        for k in range(plan.data, plan.blocks):
            out_ref[x, k * probes : (k + 1) * probes, :] = table if k == plan.blocks - 2 else zero
    return total[:, plan.left_pad :]


def first_right(plan, a, b, c, l_ref, out_ref):
    right_body(plan, a, b, c, l_ref, out_ref)


def last_right(plan, a, b, c, l_ref, out_ref, q_ref):
    q_ref[...] = right_body(plan, a, b, c, l_ref, out_ref)


def sum_parts(in_ref, out_ref):
    total = in_ref[0]
    for j in range(1, in_ref.shape[0]):
        total = total + in_ref[j]
    out_ref[...] = total


def sum_copies(exact, probes, last_ref, in_ref, out_ref):
    total = in_ref[0]
    for j in range(1, in_ref.shape[0]):
        total = total + in_ref[j]
    if not exact:
        n = total.shape[0]
        high = total[n - 2 * probes : n - probes]
        low = high - high.astype(BF16).astype(F32)
        is_last = last_ref[...] > 0.5
        tail = jnp.where(is_last, low, total[n - probes :])
        total = jnp.concatenate([total[: n - probes], tail], axis=0).astype(BF16)
    for j in range(out_ref.shape[0]):
        out_ref[j] = total


def last_squares(plan, v_ref, out_ref):
    probes = v_ref.shape[1] // plan.blocks
    squares = []
    for m in range(len(plan.outs)):
        v = vector_of(plan, v_ref, m, probes)
        squares.append(jnp.sum(v * v, axis=1, keepdims=True))
    table = lane_table(squares, probes)
    for j in range(plan.cols):
        out_ref[j] = table


def finish(plan, v1_ref, q1_ref, v2_ref, q2_ref, oa, ob, oc, sigma_ref):
    probes = q1_ref.shape[0]
    lane = lax.broadcasted_iota(jnp.int32, (probes, LANES), 1)
    outs = jnp.zeros((probes, LANES), F32) + 1.0
    ins = outs
    for m in range(len(plan.outs)):
        outs = jnp.where(lane == m, float(plan.outs[m] * plan.rows), outs)
        ins = jnp.where(lane == m, float(plan.ins[m] * plan.cols), ins)
    n = plan.blocks * probes
    t1 = v1_ref[0, n - 2 * probes : n - probes, :].astype(F32) + v1_ref[0, n - probes :, :].astype(F32)
    f1 = lax.rsqrt(t1 / outs + EPS)
    s1 = f1 * lax.rsqrt(f1 * f1 * q1_ref[...] / ins + EPS)
    t2 = v2_ref[0, n - 2 * probes : n - probes, :]
    f2 = s1 * lax.rsqrt(s1 * s1 * t2 / outs + EPS)
    q2 = q2_ref[0]
    for j in range(1, plan.cols):
        q2 = q2 + q2_ref[j]
    total = f2 * f2 * q2
    scale = f2 * lax.rsqrt(total / ins + EPS)
    sigma_ref[...] = jnp.sqrt(total / outs)
    m = 0
    for ref in (oa, ob, oc):
        for k in range(ref.shape[0]):
            part, first = plan.where[m]
            for b in range(plan.ins[m] // LANES):
                at = (first + b) * probes
                ref[k, :, b * LANES : (b + 1) * LANES] = (
                    v2_ref[part, at : at + probes, :] * scale[:, m : m + 1]
                )
            m += 1


def swap(v, axis):
    return lax.all_to_all(v, axis, 0, 0, tiled=True)


def body(gate_up, down_weight, query_output, probe_gate, probe_down, probe_query):
    xs, zs, cols = lax.axis_size("x"), lax.axis_size("z"), lax.axis_size("col")
    flat = lambda w: w.reshape(-1, *w.shape[-2:])
    weights = tuple(flat(w) for w in (gate_up, down_weight, query_output))
    vectors = tuple(flat(v) for v in (probe_gate, probe_down, probe_query))
    probes = vectors[0].shape[1]
    plan = Plan(weights, xs, zs, cols)
    bind = lambda f, *rest: functools.partial(f, *rest)
    height = plan.blocks * probes
    mine = plan.mine * probes
    left_shape = sds((cols, probes, plan.left_width), F32)
    right_shape = sds((xs, height, LANES), F32)
    is_last = jnp.broadcast_to(
        (lax.axis_index("z") == zs - 1).astype(F32), (probes, LANES)
    )

    def reduce_row(right, exact):
        right = swap(right, "x")
        right = call(sum_parts, sds((height, LANES), F32), right)
        right = swap(right.reshape(zs, mine, LANES), "z")
        out = sds((zs, mine, LANES), F32 if exact else BF16)
        right = call(bind(sum_copies, exact, probes), out, is_last, right)
        right = swap(right, "z").reshape(1, height, LANES)
        return swap(jnp.broadcast_to(right, (xs, height, LANES)), "x")

    left = call(bind(first_left, plan), left_shape, *weights, *vectors)
    left = swap(left, "col")
    right = call(bind(first_right, plan), right_shape, *weights, left)
    v1 = reduce_row(right, False)
    left = call(bind(next_left, plan), left_shape, *weights, v1)
    left = swap(left, "col")
    right, q1 = call(
        bind(last_right, plan), (right_shape, sds((probes, LANES), F32)), *weights, left
    )
    v2 = reduce_row(right, True)
    q2 = call(bind(last_squares, plan), sds((cols, probes, LANES), F32), v2)
    q2 = swap(q2, "col")
    outs = tuple(sds(v.shape, F32) for v in vectors) + (sds((probes, LANES), F32),)
    oa, ob, oc, sigma = call(bind(finish, plan), outs, v1, q1, v2, q2)
    na, nb, nc = (w.shape[0] for w in weights)
    sigma = sigma.T
    sa, sb, sc = sigma[:na], sigma[na : na + nb], sigma[na + nb : na + nb + nc]
    like = lambda s, p: s.reshape(p.shape[:-1])
    return (
        oa.reshape(probe_gate.shape),
        ob.reshape(probe_down.shape),
        oc.reshape(probe_query.shape),
        like(sa, probe_gate),
        like(sb, probe_down),
        like(sc, probe_query),
    )


def solution(mesh):
    z = 16
    finer = Mesh(mesh.devices.reshape(z, -1, mesh.shape["col"]), ("z", "x", "col"))
    row = ("z", "x")
    in_specs = (
        P(None, None, row, "col"),
        P(None, row, "col"),
        P(None, None, row, "col"),
        P(None, None, None, "col"),
        P(None, None, "col"),
        P(None, None, None, "col"),
    )
    out_specs = (
        P(None, None, None, "col"),
        P(None, None, "col"),
        P(None, None, None, "col"),
        P(),
        P(),
        P(),
    )
    return jax.shard_map(body, mesh=finer, in_specs=in_specs, out_specs=out_specs, check_vma=False)
```

time: 719 us -> 255 us (0.35)
  waiting for transfers between devices: 439 us -> 12.7 us
  blocking collectives: 114 us -> 197 us
  starting transfers between devices: 80.4 us -> 9.87 us
  other arithmetic: 32.7 us -> 0 us
  Pallas kernels: 0 us -> 28.9 us
  local copies, waits for them, and re-layouts: 22.5 us -> 4.43 us
  matrix products: 14.6 us -> 0 us
  between operations: 14.3 us -> 0.67 us
    psum x2 -> x0, waiting for transfers between devices: 406 us -> none  [body(): raw_sums = lax.psum(right_partial, ROW)]
    all_to_all x0 -> x10, blocking collectives: none -> 197 us  [swap(): return lax.all_to_all(v, axis, 0, 0, tiled=True)]
    psum x4 -> x0, blocking collectives: 114 us -> none  [over_axes(): shard = lax.psum(shard, axis)]
    all_to_all x12 -> x1, starting transfers between devices: 80.4 us -> 9.87 us  [swap(): return lax.all_to_all(v, axis, 0, 0, tiled=True)]
    pallas_call x0 -> x10, Pallas kernels: none -> 28.9 us  [call(): pl.pallas_call(kernel, out_shape=outs, in_specs=[VMEM] * len(args), out_s...]
    all_to_all x12 -> x1, waiting for transfers between devices: 32.5 us -> 12.7 us  [swap(): return lax.all_to_all(v, axis, 0, 0, tiled=True)]
    reduce_sum x24 -> x0, other arithmetic: 15.2 us -> none  [the longest x12 7.69 us: of_everyone(): return jnp.sum(everything, axis=0)]
    dot_general x12 -> x0, matrix products: 14.6 us -> none  [the longest x6 7.44 us: body(): jnp.einsum('lmoi,lmko->lmki', weight, left, preferred_element_type=jnp.fl...]
  transfers between devices with their start and end apart: 14 -> 1, of which waited for: 13 -> 1; matrix products, arithmetic and copies ran while one was open for 7% -> 0% of each run, Pallas kernels for 0% -> 0%
where the time goes in v1:
time: 255 us; the launch traced here: 253 us
  blocking collectives  197 us (77%)
  Pallas kernels  28.9 us (11%)
  waiting for transfers between devices  12.7 us (5%)
  starting transfers between devices  9.87 us (4%)
  local copies, waits for them, and re-layouts  4.43 us (2%)
    all_to_all x10, blocking collectives, swap(): return lax.all_to_all(v, axis, 0, 0, tiled=True)  197 us
    pallas_call x10, Pallas kernels, call(): pl.pallas_call(kernel, out_shape=outs, in_specs=[VMEM] * len(args), out_s...  28.9 us
    all_to_all x1, waiting for transfers between devices, swap(): return lax.all_to_all(v, axis, 0, 0, tiled=True)  12.7 us
    all_to_all x1, starting transfers between devices, swap(): return lax.all_to_all(v, axis, 0, 0, tiled=True)  9.87 us
  transfers between devices with their start and end apart: 1, of which 1 were waited for; matrix products, arithmetic and copies ran while one was open for 0% of the time, Pallas kernels for 0%

profile of v1, /device:TPU:1, one launch (start us, length us, event | category | flops | bytes accessed | tf_op | source)
XLA Modules:
  0.0 253.1 jit_solution(16411630944756249654)
XLA Ops:
  0.6 4.1 %shard_map.109 = f32[8,16,2688]{2,1,0:T(8,128)} custom-call(bf16[8,224,512]{2,1,0:T(8,128)(2,1)} %bitcast.13, bf16[4,64,1792]{2,1,0:T(8,128)(2,1)} %b.7, bf16[8,64,512]{2,1,0:T(8,128)(2,1)} %bitcast.17, bf16[8,16,512]{2,1,0:T(8,128)(2,1)} %bitcast.25, bf16[4,16,1792]{2,1,0:T(8,128)(2,1)} %vb.1, bf16[8,16,512]{2,1,0:T(8,128)(2,1)} %bitcast.26), custom_call_target="tpu_custom_call" | custom-call | tf_op jit(solution)/shard_map/pallas_call | solution.py:19
  4.8 29.8 %all_to_all.55.l_ref = f32[8,16,2688]{2,1,0:T(8,128)} all-to-all(f32[8,16,2688]{2,1,0:T(8,128)} %shard_map.109), channel_id=1, replica_groups=mesh['z'=16,'x'=4,'col'=8] {'col'}, dimensions={0} | all-to-all | bytes 2752512 | tf_op jit(solution)/shard_map/all_to_all | solution.py:215
  34.6 4.4 %shard_map.110 = f32[4,512,128]{2,1,0:T(8,128)} custom-call(bf16[8,224,512]{2,1,0:T(8,128)(2,1)} %bitcast.14, bf16[4,64,1792]{2,1,0:T(8,128)(2,1)} %b.7, bf16[8,64,512]{2,1,0:T(8,128)(2,1)} %bitcast.18, f32[8,16,2688]{2,1,0:T(8,128)} %all_to_all.55.l_ref), custom_call_target="tpu_custom_call" | custom-call | tf_op jit(solution)/shard_map/pallas_call | solution.py:19
  39.0 18.5 %all_to_all.56.in_ref = f32[4,512,128]{2,1,0:T(8,128)} all-to-all(f32[4,512,128]{2,1,0:T(8,128)} %shard_map.110), channel_id=1, replica_groups=mesh['z'=16,'x'=4,'col'=8] {'x'}, dimensions={0} | all-to-all | bytes 2097152 | tf_op jit(solution)/shard_map/all_to_all | solution.py:215
  57.4 2.0 shard_map.111
  59.4 9.9 %all-to-all-start.2 = ((f32[16,32,128]{2,1,0:T(8,128)}), f32[16,32,128]{2,1,0:T(8,128)S(1)}, u32[]{:S(2)}, u32[]{:S(2)}) async-start(f32[16,32,128]{2,1,0:T(8,128)} %bitcast.21), calls=%async_computation.2 | async-start | bytes 524288 | tf_op jit(solution)/shard_map/all_to_all | solution.py:215
  69.3 12.7 %all-to-all-done.2.in_ref = f32[16,32,128]{2,1,0:T(8,128)S(1)} async-done(((f32[16,32,128]{2,1,0:T(8,128)}), f32[16,32,128]{2,1,0:T(8,128)S(1)}, u32[]{:S(2)}, u32[]{:S(2)}) %all-to-all-start.2) | async-done | bytes 262176 | tf_op jit(solution)/shard_map/all_to_all | solution.py:215
  82.7 1.6 shard_map.112
  84.4 22.0 %all_to_all.57 = bf16[16,32,128]{2,1,0:T(8,128)(2,1)S(1)} all-to-all(bf16[16,32,128]{2,1,0:T(8,128)(2,1)} %shard_map.112), channel_id=1, replica_groups=mesh['z'=16,'x'=4,'col'=8] {'z'}, dimensions={0} | all-to-all | bytes 262144 | tf_op jit(solution)/shard_map/all_to_all | solution.py:215
  106.4 10.0 %all_to_all.58.v_ref.v1_ref = bf16[4,512,128]{2,1,0:T(8,128)(2,1)} all-to-all(bf16[4,512,128]{2,1,0:T(8,128)(2,1)S(1)} %broadcast_in_dim.19), channel_id=1, replica_groups=mesh['z'=16,'x'=4,'col'=8] {'x'}, dimensions={0} | all-to-all | bytes 1048576 | tf_op jit(solution)/shard_map/all_to_all | solution.py:215
  116.4 4.2 %shard_map.113 = f32[8,16,2688]{2,1,0:T(8,128)} custom-call(bf16[8,224,512]{2,1,0:T(8,128)(2,1)} %bitcast.15, bf16[4,64,1792]{2,1,0:T(8,128)(2,1)} %b.7, bf16[8,64,512]{2,1,0:T(8,128)(2,1)} %bitcast.19, bf16[4,512,128]{2,1,0:T(8,128)(2,1)} %all_to_all.58.v_ref.v1_ref), custom_call_target="tpu_custom_call" | custom-call | tf_op jit(solution)/shard_map/pallas_call | solution.py:19
  120.6 28.0 %all_to_all.59.l_ref = f32[8,16,2688]{2,1,0:T(8,128)} all-to-all(f32[8,16,2688]{2,1,0:T(8,128)} %shard_map.113), channel_id=1, replica_groups=mesh['z'=16,'x'=4,'col'=8] {'col'}, dimensions={0} | all-to-all | bytes 2752512 | tf_op jit(solution)/shard_map/all_to_all | solution.py:215
  148.6 4.4 %shard_map.114 = (f32[4,512,128]{2,1,0:T(8,128)}, f32[16,128]{1,0:T(8,128)}) custom-call(bf16[8,224,512]{2,1,0:T(8,128)(2,1)} %bitcast.16, bf16[4,64,1792]{2,1,0:T(8,128)(2,1)} %b.7, bf16[8,64,512]{2,1,0:T(8,128)(2,1)} %bitcast.20, f32[8,16,2688]{2,1,0:T(8,128)} %all_to_all.59.l_ref), custom_call_target="tpu_custom_call" | custom-call | tf_op jit(solution)/shard_map/pallas_call | solution.py:19
  152.9 18.5 %all_to_all.60.in_ref = f32[4,512,128]{2,1,0:T(8,128)} all-to-all(f32[4,512,128]{2,1,0:T(8,128)} %get-tuple-element.13), channel_id=1, replica_groups=mesh['z'=16,'x'=4,'col'=8] {'x'}, dimensions={0} | all-to-all | bytes 2097152 | tf_op jit(solution)/shard_map/all_to_all | solution.py:215
  171.4 2.0 shard_map.115
  173.4 16.9 %all_to_all.61.in_ref = f32[16,32,128]{2,1,0:T(8,128)} all-to-all(f32[16,32,128]{2,1,0:T(8,128)} %bitcast.22), channel_id=1, replica_groups=mesh['z'=16,'x'=4,'col'=8] {'z'}, dimensions={0} | all-to-all | bytes 524288 | tf_op jit(solution)/shard_map/all_to_all | solution.py:215
  190.3 1.7 shard_map.116
  192.0 23.1 %all_to_all.62 = f32[16,32,128]{2,1,0:T(8,128)S(1)} all-to-all(f32[16,32,128]{2,1,0:T(8,128)} %shard_map.116), channel_id=1, replica_groups=mesh['z'=16,'x'=4,'col'=8] {'z'}, dimensions={0} | all-to-all | bytes 524288 | tf_op jit(solution)/shard_map/all_to_all | solution.py:215
  215.2 12.9 %all_to_all.63.v_ref.v2_ref = f32[4,512,128]{2,1,0:T(8,128)} all-to-all(f32[4,512,128]{2,1,0:T(8,128)S(1)} %broadcast_in_dim.21), channel_id=1, replica_groups=mesh['z'=16,'x'=4,'col'=8] {'x'}, dimensions={0} | all-to-all | bytes 2097152 | tf_op jit(solution)/shard_map/all_to_all | solution.py:215
  228.0 2.0 shard_map.117
  230.0 16.9 %all_to_all.64.q2_ref = f32[8,16,128]{2,1,0:T(8,128)} all-to-all(f32[8,16,128]{2,1,0:T(8,128)} %shard_map.117), channel_id=1, replica_groups=mesh['z'=16,'x'=4,'col'=8] {'col'}, dimensions={0} | all-to-all | bytes 131072 | tf_op jit(solution)/shard_map/all_to_all | solution.py:215
  247.0 2.5 shard_map.118
  249.5 0.8 slice.13
  250.2 0.8 fusion
  (8 shorter events, 2.8 us)
Async XLA Ops:
  59.4 22.6 %all-to-all-start.2 = ((f32[16,32,128]{2,1,0:T(8,128)}), f32[16,32,128]{2,1,0:T(8,128)S(1)}, u32[]{:S(2)}, u32[]{:S(2)}) async-start(f32[16,32,128]{2,1,0:T(8,128)} %bitcast.21), calls=%async_computation.2 | async-start | bytes 524288 | tf_op jit(solution)/shard_map/all_to_all | solution.py:215
  82.0 0.7 copy-start

commit v2 on v1

v2 whole, which is shorter than its diff:
```python
import functools

import jax
import jax.numpy as jnp
from jax import lax
from jax.experimental import pallas as pl
from jax.experimental.pallas import tpu as pltpu
from jax.sharding import Mesh
from jax.sharding import PartitionSpec as P

F32 = jnp.float32
BF16 = jnp.bfloat16
EPS = 1e-06
VMEM = pl.BlockSpec(memory_space=pltpu.VMEM)
LANES = 128
LIMIT = 16 * 2**20
LEFT1, RIGHT1 = BF16, BF16
LEFT2, RIGHT2, GATHER2 = BF16, F32, BF16


def call(kernel, outs, *args):
    return pl.pallas_call(
        kernel,
        out_shape=outs,
        in_specs=[VMEM] * len(args),
        out_specs=jax.tree.map(lambda _: VMEM, outs),
        compiler_params=pltpu.CompilerParams(vmem_limit_bytes=LIMIT),
    )(*args)


def sds(shape, dtype):
    return jax.ShapeDtypeStruct(shape, dtype)


class Plan:
    def __init__(self, weights, xs, zs, cols):
        self.xs, self.zs, self.cols = xs, zs, cols
        self.rows = xs * zs
        self.outs = []
        self.ins = []
        self.where = []
        used = [0] * xs
        place = [0] * xs
        for w in weights:
            out, inp = w.shape[-2:]
            count = w.size // (out * inp)
            per = count // xs
            for m in range(count):
                part = m // per
                self.where.append((part, used[part], place[part]))
                used[part] += inp // LANES
                place[part] += 1
                self.outs.append(out)
                self.ins.append(inp)
        self.data = max(used)
        self.blocks = -(-(self.data + 2) // zs) * zs
        self.mine = self.blocks // zs
        self.left = []
        at = 0
        for out in self.outs:
            self.left.append(at)
            at += out
        self.left_end = at
        self.left_pad = -(-at // LANES) * LANES
        self.part = [
            (first, self.ins[m] // LANES)
            for m, (part, first, _) in enumerate(self.where)
            if part == 0
        ]


def matrix_of(refs, m):
    for ref in refs:
        n = ref.shape[0] * (ref.shape[1] if ref.ndim == 4 else 1)
        if m < n:
            return ref[m // ref.shape[1], m % ref.shape[1]] if ref.ndim == 4 else ref[m]
        m -= n


def lane_table(columns, probes):
    lane = lax.broadcasted_iota(jnp.int32, (probes, LANES), 1)
    table = jnp.zeros((probes, LANES), F32)
    for m, column in enumerate(columns):
        table = jnp.where(lane == m, column, table)
    return table


def pieces(table, dtype):
    high = table.astype(dtype)
    return high, (table - high.astype(F32)).astype(dtype)


def put_left(plan, lefts, table, out_ref):
    dtype = out_ref.dtype
    whole = jnp.concatenate(lefts, axis=1)
    pad = plan.left_pad - plan.left_end
    if pad:
        whole = jnp.concatenate([whole, jnp.zeros((whole.shape[0], pad), F32)], axis=1)
    whole = whole.astype(dtype)
    if table is not None:
        whole = jnp.concatenate([whole, *pieces(table, dtype)], axis=1)
    for j in range(plan.cols):
        out_ref[j] = whole


def dot_left(v, w):
    return lax.dot_general(v, w, (((1,), (1,)), ((), ())), preferred_element_type=F32)


def first_left(plan, a, b, c, va, vb, vc, out_ref):
    weights, probes = (a, b, c), (va, vb, vc)
    lefts = []
    for m in range(len(plan.outs)):
        lefts.append(dot_left(matrix_of(probes, m), matrix_of(weights, m)))
    put_left(plan, lefts, None, out_ref)


def vector_of(plan, v_ref, m, probes):
    part, first, _ = plan.where[m]
    n = plan.ins[m] // LANES
    return jnp.concatenate(
        [v_ref[part, (first + k) * probes : (first + k + 1) * probes, :] for k in range(n)], axis=1
    )


def next_left(plan, a, b, c, v_ref, out_ref):
    weights = (a, b, c)
    probes = v_ref.shape[1] // plan.blocks
    lefts, squares = [], []
    for m in range(len(plan.outs)):
        v = vector_of(plan, v_ref, m, probes)
        wide = v.astype(F32)
        squares.append(jnp.sum(wide * wide, axis=1, keepdims=True))
        lefts.append(dot_left(v, matrix_of(weights, m)))
    put_left(plan, lefts, lane_table(squares, probes), out_ref)


def sum_of(ref):
    total = ref[0].astype(F32)
    for j in range(1, ref.shape[0]):
        total = total + ref[j].astype(F32)
    return total


def right_body(plan, a, b, c, l_ref, out_ref, exact):
    weights = (a, b, c)
    total = sum_of(l_ref)
    probes = total.shape[0]
    dtype = out_ref.dtype
    squares = []
    for m in range(len(plan.outs)):
        raw = total[:, plan.left[m] : plan.left[m] + plan.outs[m]]
        squares.append(jnp.sum(raw * raw, axis=1, keepdims=True))
        weight = matrix_of(weights, m)
        high, low = pieces(raw, BF16)
        right = jnp.dot(high, weight, preferred_element_type=F32)
        if exact:
            right = right + jnp.dot(low, weight, preferred_element_type=F32)
        right = right.astype(dtype)
        part, first, _ = plan.where[m]
        for k in range(plan.ins[m] // LANES):
            at = (first + k) * probes
            out_ref[part, at : at + probes, :] = right[:, k * LANES : (k + 1) * LANES]
    high, low = pieces(lane_table(squares, probes), dtype)
    zero = jnp.zeros((probes, LANES), dtype)
    for x in range(plan.xs):
        for k in range(plan.data, plan.blocks):
            value = {plan.blocks - 2: high, plan.blocks - 1: low}.get(k, zero)
            out_ref[x, k * probes : (k + 1) * probes, :] = value
    return total


def first_right(plan, a, b, c, l_ref, out_ref):
    right_body(plan, a, b, c, l_ref, out_ref, False)


def last_right(plan, a, b, c, l_ref, out_ref, q_ref):
    total = right_body(plan, a, b, c, l_ref, out_ref, True)
    at = plan.left_pad
    q_ref[...] = total[:, at : at + LANES] + total[:, at + LANES :]


def tail_pieces(total, probes, dtype):
    n = total.shape[0]
    table = total[n - 2 * probes : n - probes] + total[n - probes :]
    return pieces(table, dtype)


def sum_parts(probes, in_ref, out_ref):
    total = sum_of(in_ref)
    n = total.shape[0]
    out_ref[...] = total.astype(out_ref.dtype)
    high, low = tail_pieces(total, probes, out_ref.dtype)
    out_ref[n - 2 * probes : n - probes, :] = high
    out_ref[n - probes :, :] = low


def sum_copies(probes, zs, in_ref, out_ref):
    total = sum_of(in_ref)
    n = total.shape[0]
    dtype = out_ref.dtype
    last = lax.axis_index("z") == zs - 1
    high, low = tail_pieces(total, probes, dtype)
    rounded = total.astype(dtype)
    for j in range(zs):
        out_ref[j] = rounded

    @pl.when(last)
    def _():
        for j in range(zs):
            out_ref[j, n - 2 * probes : n - probes, :] = high
            out_ref[j, n - probes :, :] = low


def part_squares(plan, v_ref, out_ref):
    probes = v_ref.shape[0] // plan.blocks
    columns = []
    for first, n in plan.part:
        total = jnp.zeros((probes, 1), F32)
        for k in range(first, first + n):
            v = v_ref[k * probes : (k + 1) * probes, :].astype(F32)
            total = total + jnp.sum(v * v, axis=1, keepdims=True)
        columns.append(total)
    table = lane_table(columns, probes)
    for j in range(out_ref.shape[0]):
        out_ref[j] = table


def finish(plan, v1_ref, q1_ref, v2_ref, q2_ref, oa, ob, oc, sa, sb, sc):
    probes = q1_ref.shape[0]
    lane = lax.broadcasted_iota(jnp.int32, (probes, LANES), 1)
    outs = jnp.zeros((probes, LANES), F32) + 1.0
    ins = outs
    for m in range(len(plan.outs)):
        outs = jnp.where(lane == m, float(plan.outs[m] * plan.rows), outs)
        ins = jnp.where(lane == m, float(plan.ins[m] * plan.cols), ins)
    n = plan.blocks * probes
    t1 = v1_ref[0, n - 2 * probes : n - probes, :].astype(F32) + v1_ref[0, n - probes :, :].astype(F32)
    f1 = lax.rsqrt(t1 / outs + EPS)
    s1 = f1 * lax.rsqrt(f1 * f1 * q1_ref[...] / ins + EPS)
    t2 = v2_ref[0, n - 2 * probes : n - probes, :].astype(F32) + v2_ref[0, n - probes :, :].astype(F32)
    f2 = s1 * lax.rsqrt(s1 * s1 * t2 / outs + EPS)
    by_part = []
    for x in range(plan.xs):
        q = q2_ref[x * plan.cols]
        for j in range(1, plan.cols):
            q = q + q2_ref[x * plan.cols + j]
        by_part.append(q)
    q2 = lane_table([by_part[part][:, i : i + 1] for part, _, i in plan.where], probes)
    total = f2 * f2 * q2
    scale = f2 * lax.rsqrt(total / ins + EPS)
    sigma = jnp.sqrt(total / outs).T
    m = 0
    for ref, sig in ((oa, sa), (ob, sb), (oc, sc)):
        n1, n2 = (ref.shape[0], 1) if ref.ndim == 3 else ref.shape[:2]
        if sig.ndim == 2:
            sig[...] = sigma[m : m + n1]
        else:
            for k in range(n1):
                sig[k] = sigma[m + k * n2 : m + (k + 1) * n2]
        for k in range(n1 * n2):
            part, first, _ = plan.where[m]
            for b in range(plan.ins[m] // LANES):
                at = (first + b) * probes
                value = v2_ref[part, at : at + probes, :].astype(F32) * scale[:, m : m + 1]
                here = slice(b * LANES, (b + 1) * LANES)
                if ref.ndim == 3:
                    ref[k, :, here] = value
                else:
                    ref[k // n2, k % n2, :, here] = value
            m += 1


def swap(v, axis):
    return lax.all_to_all(v, axis, 0, 0, tiled=True)


def body(gate_up, down_weight, query_output, probe_gate, probe_down, probe_query):
    xs, zs, cols = lax.axis_size("x"), lax.axis_size("z"), lax.axis_size("col")
    weights = (gate_up, down_weight, query_output)
    vectors = (probe_gate, probe_down, probe_query)
    probes = probe_down.shape[1]
    plan = Plan(weights, xs, zs, cols)
    bind = lambda f, *rest: functools.partial(f, *rest)
    height = plan.blocks * probes
    mine = plan.mine * probes

    def left_shape(extra, dtype):
        return sds((cols, probes, plan.left_pad + extra * LANES), dtype)

    def right_shape(dtype):
        return sds((xs, height, LANES), dtype)

    def reduce_row(right, gather):
        right = swap(right, "x")
        right = call(bind(sum_parts, probes), sds((height, LANES), right.dtype), right)
        right = swap(right.reshape(zs, mine, LANES), "z")
        right = call(bind(sum_copies, probes, zs), sds((zs, mine, LANES), gather), right)
        return swap(right, "z").reshape(height, LANES)

    def all_parts(right):
        return swap(jnp.broadcast_to(right[None], (xs, height, LANES)), "x")

    left = call(bind(first_left, plan), left_shape(0, LEFT1), *weights, *vectors)
    left = swap(left, "col")
    right = call(bind(first_right, plan), right_shape(RIGHT1), *weights, left)
    v1 = all_parts(reduce_row(right, BF16))
    left = call(bind(next_left, plan), left_shape(2, LEFT2), *weights, v1)
    left = swap(left, "col")
    right, q1 = call(
        bind(last_right, plan), (right_shape(RIGHT2), sds((probes, LANES), F32)), *weights, left
    )
    part = reduce_row(right, GATHER2)
    q2 = call(bind(part_squares, plan), sds((xs * cols, probes, LANES), F32), part)
    q2 = swap(q2, ("x", "col"))
    v2 = all_parts(part)
    outs = tuple(sds(v.shape, F32) for v in vectors)
    outs += tuple(sds(v.shape[:-1], F32) for v in vectors)
    return call(bind(finish, plan), outs, v1, q1, v2, q2)


def solution(mesh):
    z = 16
    finer = Mesh(mesh.devices.reshape(z, -1, mesh.shape["col"]), ("z", "x", "col"))
    row = ("z", "x")
    in_specs = (
        P(None, None, row, "col"),
        P(None, row, "col"),
        P(None, None, row, "col"),
        P(None, None, None, "col"),
        P(None, None, "col"),
        P(None, None, None, "col"),
    )
    out_specs = (
        P(None, None, None, "col"),
        P(None, None, "col"),
        P(None, None, None, "col"),
        P(),
        P(),
        P(),
    )
    return jax.shard_map(body, mesh=finer, in_specs=in_specs, out_specs=out_specs, check_vma=False)
```

time: 255 us -> 197 us (0.77)
  Pallas kernels: 28.9 us -> 5.64 us
  blocking collectives: 197 us -> 183 us
  waiting for transfers between devices: 12.7 us -> 0 us
  starting transfers between devices: 9.87 us -> 0 us
    pallas_call x10, Pallas kernels: 28.9 us -> 5.64 us  [call(): pl.pallas_call(kernel, out_shape=outs, in_specs=[VMEM] * len(args), out_s...]
    all_to_all x10 -> x11, blocking collectives: 197 us -> 183 us  [swap(): return lax.all_to_all(v, axis, 0, 0, tiled=True)]
    all_to_all x1 -> x0, waiting for transfers between devices: 12.7 us -> none  [swap(): return lax.all_to_all(v, axis, 0, 0, tiled=True)]
    all_to_all x1 -> x0, starting transfers between devices: 9.87 us -> none  [swap(): return lax.all_to_all(v, axis, 0, 0, tiled=True)]
    unnamed x3 -> x14, local copies, waits for them, and re-layouts: 0.73 us -> 6.46 us
    slice x4 -> x0, local copies, waits for them, and re-layouts: 2.93 us -> none  [body(): sa, sb, sc = (sigma[:na], sigma[na:na + nb], sigma[na + nb:na + nb + nc])]
  transfers between devices with their start and end apart: 1 -> 0, of which waited for: 1 -> 0; matrix products, arithmetic and copies ran while one was open for 0% -> 0% of each run, Pallas kernels for 0% -> 0%
where the time goes in v2:
time: 197 us; the launch traced here: 196 us
  blocking collectives  183 us (93%)
  local copies, waits for them, and re-layouts  6.6 us (3%)
  Pallas kernels  5.64 us (3%)
    all_to_all x11, blocking collectives, swap(): return lax.all_to_all(v, axis, 0, 0, tiled=True)  183 us
    unnamed x14, local copies, waits for them, and re-layouts  6.46 us
    pallas_call x10, Pallas kernels, call(): pl.pallas_call(kernel, out_shape=outs, in_specs=[VMEM] * len(args), out_s...  5.64 us

profile of v2, /device:TPU:1, one launch (start us, length us, event | category | flops | bytes accessed | tf_op | source)
XLA Modules:
  0.0 196.2 jit_solution(5987484641677565387)
XLA Ops:
  0.6 1.5 copy-done
  2.1 1.2 copy-done.2
  3.3 1.0 copy-done.3
  4.4 0.9 copy-done.4
  5.3 0.9 copy-done.5
  6.2 0.9 copy-done.6
  7.1 1.0 shard_map.109
  8.1 20.1 %all_to_all.55.l_ref = bf16[8,16,2560]{2,1,0:T(8,128)(2,1)S(1)} all-to-all(bf16[8,16,2560]{2,1,0:T(8,128)(2,1)S(1)} %shard_map.109), channel_id=1, replica_groups=mesh['z'=16,'x'=4,'col'=8] {'col'}, dimensions={0} | all-to-all | bytes 1310720 | tf_op jit(solution)/shard_map/all_to_all | solution.py:275
  28.3 1.1 shard_map.110
  29.3 10.9 %all_to_all.56.in_ref = bf16[4,512,128]{2,1,0:T(8,128)(2,1)S(1)} all-to-all(bf16[4,512,128]{2,1,0:T(8,128)(2,1)S(1)} %shard_map.110), channel_id=1, replica_groups=mesh['z'=16,'x'=4,'col'=8] {'x'}, dimensions={0} | all-to-all | bytes 1048576 | tf_op jit(solution)/shard_map/all_to_all | solution.py:275
  40.4 24.6 %all_to_all.57.in_ref = bf16[16,32,128]{2,1,0:T(8,128)(2,1)S(1)} all-to-all(bf16[16,32,128]{2,1,0:T(8,128)(2,1)S(1)} %bitcast.7), channel_id=1, replica_groups=mesh['z'=16,'x'=4,'col'=8] {'z'}, dimensions={0} | all-to-all | bytes 262144 | tf_op jit(solution)/shard_map/all_to_all | solution.py:275
  65.0 16.3 %all_to_all.58 = bf16[16,32,128]{2,1,0:T(8,128)(2,1)S(1)} all-to-all(bf16[16,32,128]{2,1,0:T(8,128)(2,1)S(1)} %shard_map.112), channel_id=1, replica_groups=mesh['z'=16,'x'=4,'col'=8] {'z'}, dimensions={0} | all-to-all | bytes 262144 | tf_op jit(solution)/shard_map/all_to_all | solution.py:275
  81.3 0.1 broadcast_in_dim.15
  81.4 9.3 %all_to_all.59.v_ref.v1_ref = bf16[4,512,128]{2,1,0:T(8,128)(2,1)S(1)} all-to-all(bf16[4,512,128]{2,1,0:T(8,128)(2,1)S(1)} %broadcast_in_dim.15), channel_id=1, replica_groups=mesh['z'=16,'x'=4,'col'=8] {'x'}, dimensions={0} | all-to-all | bytes 1048576 | tf_op jit(solution)/shard_map/all_to_all | solution.py:275
  90.7 1.0 shard_map.113
  91.8 19.4 %all_to_all.60.l_ref = bf16[8,16,2816]{2,1,0:T(8,128)(2,1)S(1)} all-to-all(bf16[8,16,2816]{2,1,0:T(8,128)(2,1)S(1)} %shard_map.113), channel_id=1, replica_groups=mesh['z'=16,'x'=4,'col'=8] {'col'}, dimensions={0} | all-to-all | bytes 1441792 | tf_op jit(solution)/shard_map/all_to_all | solution.py:275
  111.1 1.0 shard_map.114
  112.2 16.7 %all_to_all.61.in_ref = f32[4,512,128]{2,1,0:T(8,128)S(1)} all-to-all(f32[4,512,128]{2,1,0:T(8,128)S(1)} %get-tuple-element.9), channel_id=1, replica_groups=mesh['z'=16,'x'=4,'col'=8] {'x'}, dimensions={0} | all-to-all | bytes 2097152 | tf_op jit(solution)/shard_map/all_to_all | solution.py:275
  128.9 16.1 %all_to_all.62.in_ref = f32[16,32,128]{2,1,0:T(8,128)S(1)} all-to-all(f32[16,32,128]{2,1,0:T(8,128)S(1)} %bitcast.6), channel_id=1, replica_groups=mesh['z'=16,'x'=4,'col'=8] {'z'}, dimensions={0} | all-to-all | bytes 524288 | tf_op jit(solution)/shard_map/all_to_all | solution.py:275
  145.0 22.1 %all_to_all.63 = bf16[16,32,128]{2,1,0:T(8,128)(2,1)S(1)} all-to-all(bf16[16,32,128]{2,1,0:T(8,128)(2,1)S(1)} %shard_map.116), channel_id=1, replica_groups=mesh['z'=16,'x'=4,'col'=8] {'z'}, dimensions={0} | all-to-all | bytes 262144 | tf_op jit(solution)/shard_map/all_to_all | solution.py:275
  167.1 0.2 shard_map.117
  167.3 16.0 %all_to_all.64.q2_ref = f32[32,16,128]{2,1,0:T(8,128)S(1)} all-to-all(f32[32,16,128]{2,1,0:T(8,128)S(1)} %shard_map.117), channel_id=1, replica_groups=mesh['z'=16,'x'=4,'col'=8] {'x','col'}, dimensions={0} | all-to-all | bytes 524288 | tf_op jit(solution)/shard_map/all_to_all | solution.py:275
  183.3 11.7 %all_to_all.65.v2_ref = bf16[4,512,128]{2,1,0:T(8,128)(2,1)S(1)} all-to-all(bf16[4,512,128]{2,1,0:T(8,128)(2,1)S(1)} %broadcast_in_dim.17), channel_id=1, replica_groups=mesh['z'=16,'x'=4,'col'=8] {'x'}, dimensions={0} | all-to-all | bytes 1048576 | tf_op jit(solution)/shard_map/all_to_all | solution.py:275
  195.0 1.2 shard_map.118
  (13 shorter events, 0.3 us)
Async XLA Ops:
  0.6 1.5 copy-start
  2.1 1.2 copy-start.2
  3.3 1.0 copy-start.3
  4.4 0.9 copy-start.4
  5.3 0.9 copy-start.5
  6.2 0.9 copy-start.6
  40.3 50.5 %copy-start.1 = (bf16[4,2,224,512]{3,2,1,0:T(8,128)(2,1)S(1)}, bf16[4,2,224,512]{3,2,1,0:T(8,128)(2,1)}, u32[]{:S(2)}) copy-start(bf16[4,2,224,512]{3,2,1,0:T(8,128)(2,1)} %a.7) | copy-start | bytes 5505028

commit v3 on v2

v3 whole, which is shorter than its diff:
```python
import functools

import jax
import jax.numpy as jnp
from jax import lax
from jax.experimental import pallas as pl
from jax.experimental.pallas import tpu as pltpu
from jax.sharding import Mesh
from jax.sharding import PartitionSpec as P

F32 = jnp.float32
BF16 = jnp.bfloat16
EPS = 1e-06
VMEM = pl.BlockSpec(memory_space=pltpu.VMEM)
LANES = 128
LIMIT = 16 * 2**20
WIRE = jnp.float16
TAIL = BF16
SECOND = 8
TOP = 2.0**15
HBM = pl.BlockSpec(memory_space=pltpu.HBM)


def call(kernel, outs, *args, specs=None, scratch=()):
    return pl.pallas_call(
        kernel,
        out_shape=outs,
        in_specs=specs or [VMEM] * len(args),
        out_specs=jax.tree.map(lambda _: VMEM, outs),
        scratch_shapes=scratch,
        compiler_params=pltpu.CompilerParams(vmem_limit_bytes=LIMIT),
    )(*args)


def sds(shape, dtype):
    return jax.ShapeDtypeStruct(shape, dtype)


class Plan:
    def __init__(self, weights, xs, zs, cols):
        self.xs, self.zs, self.cols = xs, zs, cols
        self.rows = xs * zs
        self.outs = []
        self.ins = []
        self.where = []
        used = [0] * xs
        place = [0] * xs
        for w in weights:
            out, inp = w.shape[-2:]
            count = w.size // (out * inp)
            per = count // xs
            for m in range(count):
                part = m // per
                self.where.append((part, used[part], place[part]))
                used[part] += inp // LANES
                place[part] += 1
                self.outs.append(out)
                self.ins.append(inp)
        self.data = max(used)
        assert max(place) <= SECOND
        self.blocks = self.data + 2 + (-(self.data + 2)) % 16
        self.high, self.low = self.blocks - 2, self.blocks - 1
        self.left = []
        at = 0
        for out in self.outs:
            self.left.append(at)
            at += out
        self.left_end = at
        self.left_pad = -(-at // LANES) * LANES
        self.part = [
            (first, self.ins[m] // LANES, self.ins[m])
            for m, (part, first, _) in enumerate(self.where)
            if part == 0
        ]

    def counts(self, probes):
        lane = lax.broadcasted_iota(jnp.int32, (probes, LANES), 1)
        outs = jnp.zeros((probes, LANES), F32) + 1.0
        ins = outs
        for m in range(len(self.outs)):
            outs = jnp.where(lane == m, float(self.outs[m] * self.rows), outs)
            ins = jnp.where(lane == m, float(self.ins[m] * self.cols), ins)
        return outs, ins


def matrix_of(refs, m):
    for ref in refs:
        n = ref.shape[0] * (ref.shape[1] if ref.ndim == 4 else 1)
        if m < n:
            return ref[m // ref.shape[1], m % ref.shape[1]] if ref.ndim == 4 else ref[m]
        m -= n


def lane_table(columns, rows, base=0):
    lane = lax.broadcasted_iota(jnp.int32, (rows, LANES), 1)
    table = jnp.zeros((rows, LANES), F32)
    for m, column in enumerate(columns):
        table = jnp.where(lane == m + base, column, table)
    return table


def pieces(table, dtype):
    high = table.astype(dtype)
    return high, (table - high.astype(F32)).astype(dtype)


def by_matrix(plan, parts, base=0):
    columns = [parts[part][:, base + i : base + i + 1] for part, _, i in plan.where]
    return lane_table(columns, parts[0].shape[0])


def put_left(plan, lefts, table, out_ref):
    dtype = out_ref.dtype
    whole = jnp.concatenate(lefts, axis=1)
    pad = plan.left_pad - plan.left_end
    if pad:
        whole = jnp.concatenate([whole, jnp.zeros((whole.shape[0], pad), F32)], axis=1)
    whole = jnp.concatenate([whole.astype(dtype), *pieces(table, dtype)], axis=1)
    for j in range(plan.cols):
        out_ref[j] = whole


def dot_left(v, w):
    return lax.dot_general(v, w, (((1,), (1,)), ((), ())), preferred_element_type=F32)


def first_left(plan, a, b, c, va, vb, vc, out_ref, *scratch):
    held, sems = scratch[:6], scratch[6]
    copies = []
    for k, (src, dst) in enumerate(zip((va, a, vb, b, vc, c), held)):
        copies.append(pltpu.make_async_copy(src, dst, sems.at[k]))
        copies[-1].start()
    lefts, norms = [], []
    for k in range(3):
        copies[2 * k].wait()
        copies[2 * k + 1].wait()
        probe, weight = held[2 * k], held[2 * k + 1]
        count = weight.shape[0] * (weight.shape[1] if weight.ndim == 4 else 1)
        for m in range(count):
            w = matrix_of((weight,), m)
            lefts.append(dot_left(matrix_of((probe,), m), w))
            wide = w.astype(F32)
            norms.append(jnp.sum(jnp.sum(wide * wide, axis=0, keepdims=True), axis=1, keepdims=True))
    put_left(plan, lefts, lane_table(norms, lefts[0].shape[0]), out_ref)


def vector_of(plan, v_ref, m):
    part, first, _ = plan.where[m]
    n = plan.ins[m] // LANES
    return jnp.concatenate([v_ref[part, first + k] for k in range(n)], axis=1)


def next_left(plan, a, b, c, v_ref, out_ref):
    weights = (a, b, c)
    probes = v_ref.shape[2]
    lefts, squares = [], []
    for m in range(len(plan.outs)):
        v = vector_of(plan, v_ref, m)
        wide = v.astype(F32)
        squares.append(jnp.sum(wide * wide, axis=1, keepdims=True))
        lefts.append(dot_left(v, matrix_of(weights, m)))
    put_left(plan, lefts, lane_table(squares, probes), out_ref)


def sum_of(ref):
    total = ref[0].astype(F32)
    for j in range(1, ref.shape[0]):
        total = total + ref[j].astype(F32)
    return total


def sum_left(plan, l_ref):
    total = sum_of(l_ref)
    at = plan.left_pad
    return total, total[:, at : at + LANES] + total[:, at + LANES :]


def put_right(plan, weights, total, scale, tables, out_ref, rows_ref):
    probes = total.shape[0]
    for m in range(len(plan.outs)):
        raw = total[:, plan.left[m] : plan.left[m] + plan.outs[m]]
        if scale is not None:
            raw = raw * scale[:, m : m + 1]
        weight = matrix_of(weights, m)
        high, low = pieces(raw, BF16)
        right = jnp.dot(high, weight, preferred_element_type=F32)
        right = right + jnp.dot(low, weight, preferred_element_type=F32)
        part, first, _ = plan.where[m]
        for k in range(plan.ins[m] // LANES):
            rows_ref[part, :, first + k, :] = right[:, k * LANES : (k + 1) * LANES]
    zero = jnp.zeros((probes, LANES), F32)
    for x in range(plan.xs):
        for k in range(plan.data, plan.high):
            rows_ref[x, :, k, :] = zero
        high = tables[x].astype(TAIL).astype(F32)
        rows_ref[x, :, plan.high, :] = high
        rows_ref[x, :, plan.low, :] = tables[x] - high
    if out_ref is not None:
        for x in range(plan.xs):
            out_ref[x] = rows_ref[x].astype(out_ref.dtype)


def left_squares(plan, total):
    squares = []
    for m in range(len(plan.outs)):
        raw = total[:, plan.left[m] : plan.left[m] + plan.outs[m]]
        squares.append(jnp.sum(raw * raw, axis=1, keepdims=True))
    return squares


def of_part(plan, x, columns):
    return [column for column, where in zip(columns, plan.where) if where[0] == x]


def first_right(plan, a, b, c, l_ref, out_ref, rows_ref):
    total, norms = sum_left(plan, l_ref)
    probes = total.shape[0]
    squares = left_squares(plan, total)
    norms = [norms[:, m : m + 1] for m in range(len(plan.outs))]
    tables = [
        lane_table(of_part(plan, x, squares), probes)
        + lane_table(of_part(plan, x, norms), probes, SECOND)
        for x in range(plan.xs)
    ]
    put_right(plan, (a, b, c), total, None, tables, out_ref, rows_ref)


def last_right(plan, a, b, c, l_ref, v_ref, out_ref, stats_ref):
    total, q1 = sum_left(plan, l_ref)
    probes = total.shape[0]
    outs, ins = plan.counts(probes)
    parts = [v_ref[x, plan.high].astype(F32) + v_ref[x, plan.low].astype(F32) for x in range(plan.xs)]
    t1 = by_matrix(plan, parts)
    norm = by_matrix(plan, parts, SECOND) * 1.01
    f1 = lax.rsqrt(t1 / outs + EPS)
    s1 = f1 * lax.rsqrt(f1 * f1 * q1 / ins + EPS)
    root = jnp.sqrt(q1 * 1.01 + 1e-33)
    scale = TOP / jnp.maximum(norm * root, 1e-30)
    square_scale = TOP / jnp.maximum(norm * root * root, 1e-30)
    stats_ref[0] = s1
    stats_ref[1] = scale
    stats_ref[2] = square_scale
    squares = [
        column * square_scale[:, m : m + 1] for m, column in enumerate(left_squares(plan, total))
    ]
    tables = [lane_table(of_part(plan, x, squares), probes) for x in range(plan.xs)]
    put_right(plan, (a, b, c), total, scale, tables, None, out_ref)


def split_again(plan, total, axis, dtype):
    row = lax.broadcasted_iota(jnp.int32, total.shape, axis)
    table = lax.slice_in_dim(total, plan.high, plan.high + 1, axis=axis)
    table = table + lax.slice_in_dim(total, plan.low, plan.low + 1, axis=axis)
    high = table.astype(dtype).astype(F32)
    return jnp.where(row == plan.high, high, jnp.where(row == plan.low, table - high, total))


def sum_parts(plan, in_ref, out_ref):
    dtype = out_ref.dtype
    out_ref[...] = split_again(plan, sum_of(in_ref), 1, dtype).astype(dtype)


def sum_copies(plan, in_ref, out_ref):
    dtype = out_ref.dtype
    total = split_again(plan, sum_of(in_ref), 0, dtype).astype(dtype)
    for j in range(plan.zs):
        out_ref[j] = total


def own_squares(plan, y_ref, out_ref):
    columns = []
    for first, n, _ in plan.part:
        y = y_ref[first : first + n, :]
        total = jnp.sum(y * y, axis=1, keepdims=True)
        columns.append(jnp.sum(total, axis=0, keepdims=True))
    table = lane_table(columns, out_ref.shape[1])
    for j in range(plan.cols):
        out_ref[j] = table


def unit(plan, y_ref, q_ref, out_ref):
    q = sum_of(q_ref)[:1]
    out_ref[...] = jnp.zeros(out_ref.shape, F32)
    for i, (first, n, inp) in enumerate(plan.part):
        factor = lax.rsqrt(jnp.maximum(q[:, i : i + 1] / float(inp * plan.cols), 1e-30))
        out_ref[first : first + n, :] = y_ref[first : first + n, :] * factor
    lane = lax.broadcasted_iota(jnp.int32, (1, LANES), 1)
    left = y_ref[plan.high : plan.high + 1, :] + y_ref[plan.low : plan.low + 1, :]
    left = [left[:, i : i + 1] for i in range(len(plan.part))]
    table = jnp.where(lane < SECOND, jnp.sqrt(q), lane_table(left, 1, SECOND))
    high = table.astype(TAIL).astype(F32)
    out_ref[plan.high : plan.high + 1, :] = high
    out_ref[plan.low : plan.low + 1, :] = table - high


def finish(plan, stats_ref, v_ref, oa, ob, oc, sa, sb, sc):
    probes = v_ref.shape[2]
    outs, ins = plan.counts(probes)
    parts = [v_ref[x, plan.high].astype(F32) + v_ref[x, plan.low].astype(F32) for x in range(plan.xs)]
    root = by_matrix(plan, parts)
    t2 = by_matrix(plan, parts, SECOND) / stats_ref[2]
    s1 = stats_ref[0]
    f2 = s1 * lax.rsqrt(s1 * s1 * t2 / outs + EPS)
    root = root / stats_ref[1] * f2
    spread = root * lax.rsqrt(ins)
    scale = spread * lax.rsqrt(spread * spread + EPS)
    sigma = (root * lax.rsqrt(outs)).T
    m = 0
    for ref, sig in ((oa, sa), (ob, sb), (oc, sc)):
        n1, n2 = (ref.shape[0], 1) if ref.ndim == 3 else ref.shape[:2]
        if sig.ndim == 2:
            sig[...] = sigma[m : m + n1]
        else:
            for k in range(n1):
                sig[k] = sigma[m + k * n2 : m + (k + 1) * n2]
        for k in range(n1 * n2):
            part, first, _ = plan.where[m]
            for b in range(plan.ins[m] // LANES):
                value = v_ref[part, first + b].astype(F32) * scale[:, m : m + 1]
                here = slice(b * LANES, (b + 1) * LANES)
                if ref.ndim == 3:
                    ref[k, :, here] = value
                else:
                    ref[k // n2, k % n2, :, here] = value
            m += 1


def swap(v, axis):
    return lax.all_to_all(v, axis, 0, 0, tiled=True)


def body(gate_up, down_weight, query_output, probe_gate, probe_down, probe_query):
    xs, zs, cols = lax.axis_size("x"), lax.axis_size("z"), lax.axis_size("col")
    weights = (gate_up, down_weight, query_output)
    vectors = (probe_gate, probe_down, probe_query)
    probes = probe_down.shape[1]
    plan = Plan(weights, xs, zs, cols)
    bind = lambda f, *rest: functools.partial(f, *rest)
    blocks = plan.blocks
    left_shape = sds((cols, probes, plan.left_pad + 2 * LANES), BF16)
    rows = pltpu.VMEM((xs, probes, blocks, LANES), F32)

    def right_shape(dtype):
        return sds((xs, probes, blocks, LANES), dtype)

    def gather(copies):
        part = jnp.swapaxes(swap(copies, "z"), 0, 1)
        return swap(jnp.broadcast_to(part[None], (xs, *part.shape)), "x")

    held = [pltpu.VMEM(x.shape, x.dtype) for pair in zip(vectors, weights) for x in pair]
    left = call(
        bind(first_left, plan),
        left_shape,
        *weights,
        *vectors,
        specs=[HBM] * 6,
        scratch=[*held, pltpu.SemaphoreType.DMA((6,))],
    )
    left = swap(left, "col")
    right = call(bind(first_right, plan), right_shape(BF16), *weights, left, scratch=[rows])
    right = swap(right, "x")
    right = call(bind(sum_parts, plan), sds((probes, blocks, LANES), BF16), right)
    right = swap(right, "z")
    v1 = gather(call(bind(sum_copies, plan), sds((zs, blocks, LANES), BF16), right))

    left = call(bind(next_left, plan), left_shape, *weights, v1)
    left = swap(left, "col")
    shapes = (right_shape(F32), sds((3, probes, LANES), F32))
    right, stats = call(bind(last_right, plan), shapes, *weights, left, v1)
    right = swap(right.astype(WIRE), "x")
    right = jnp.sum(right.astype(F32), axis=0).astype(WIRE)
    right = jnp.sum(swap(right, "z").astype(F32), axis=0)
    q2 = call(bind(own_squares, plan), sds((cols, 8, LANES), F32), right)
    q2 = swap(q2, "col")
    own = call(bind(unit, plan), sds((blocks, LANES), F32), right, q2)
    v2 = gather(jnp.broadcast_to(own.astype(WIRE)[None], (zs, *own.shape))).astype(F32)
    outs = tuple(sds(v.shape, F32) for v in vectors)
    outs += tuple(sds(v.shape[:-1], F32) for v in vectors)
    return call(bind(finish, plan), outs, stats, v2)


def solution(mesh):
    z = 16
    finer = Mesh(mesh.devices.reshape(z, -1, mesh.shape["col"]), ("z", "x", "col"))
    row = ("z", "x")
    in_specs = (
        P(None, None, row, "col"),
        P(None, row, "col"),
        P(None, None, row, "col"),
        P(None, None, None, "col"),
        P(None, None, "col"),
        P(None, None, None, "col"),
    )
    out_specs = (
        P(None, None, None, "col"),
        P(None, None, "col"),
        P(None, None, None, "col"),
        P(),
        P(),
        P(),
    )
    return jax.shard_map(body, mesh=finer, in_specs=in_specs, out_specs=out_specs, check_vma=False)
```

time: 197 us -> 182 us (0.924); the launches traced: 196 us -> 179 us
  blocking collectives: 183 us -> 163 us
  Pallas kernels: 5.64 us -> 7.98 us
    all_to_all x11, blocking collectives: 183 us -> 163 us  [swap(): return lax.all_to_all(v, axis, 0, 0, tiled=True)]
    pallas_call x10 -> x9, Pallas kernels: 5.64 us -> 7.98 us  [call(): pl.pallas_call(kernel, out_shape=outs, in_specs=specs or [VMEM] * len(arg...]
where the time goes in v3:
time: 182 us; the launch traced here: 179 us
  blocking collectives  163 us (90%)
  Pallas kernels  7.98 us (4%)
  local copies, waits for them, and re-layouts  6.74 us (4%)
    all_to_all x11, blocking collectives, swap(): return lax.all_to_all(v, axis, 0, 0, tiled=True)  163 us
    pallas_call x9, Pallas kernels, call(): pl.pallas_call(kernel, out_shape=outs, in_specs=specs or [VMEM] * len(arg...  7.98 us
    unnamed x14, local copies, waits for them, and re-layouts  6.46 us

profile of v3, /device:TPU:1, one launch (start us, length us, event | category | flops | bytes accessed | tf_op | source)
XLA Modules:
  0.0 178.9 jit_solution(224134364716744062)
XLA Ops:
  0.6 1.5 copy-done
  2.1 1.2 copy-done.2
  3.3 1.0 copy-done.3
  4.4 0.9 copy-done.4
  5.3 0.9 copy-done.5
  6.2 0.9 copy-done.6
  7.1 2.3 %shard_map.109 = bf16[8,16,2816]{2,1,0:T(8,128)(2,1)S(1)} custom-call(bf16[4,2,224,512]{3,2,1,0:T(8,128)(2,1)S(1)} %copy-done, bf16[4,64,1792]{2,1,0:T(8,128)(2,1)S(1)} %copy-done.2, bf16[4,2,64,512]{3,2,1,0:T(8,128)(2,1)S(1)} %copy-done.3, bf16[4,2,16,512]{3,2,1,0:T(8,128)(2,1)S(1)} %copy-done.5, bf16[4,16,1792]{2,1,0:T(8,128)(2,1)S(1)} %copy-done.4, ...), custom_call_target="tpu_custom_call" | custom-call | tf_op jit(solution)/shard_map/pallas_call | solution.py:25
  9.4 20.8 %all_to_all.55.l_ref = bf16[8,16,2816]{2,1,0:T(8,128)(2,1)S(1)} all-to-all(bf16[8,16,2816]{2,1,0:T(8,128)(2,1)S(1)} %shard_map.109), channel_id=1, replica_groups=mesh['z'=16,'x'=4,'col'=8] {'col'}, dimensions={0} | all-to-all | bytes 1441792 | tf_op jit(solution)/shard_map/all_to_all | solution.py:329
  30.2 1.3 shard_map.110
  31.5 11.0 %all_to_all.56.in_ref = bf16[4,16,32,128]{3,2,1,0:T(8,128)(2,1)S(1)} all-to-all(bf16[4,16,32,128]{3,2,1,0:T(8,128)(2,1)S(1)} %shard_map.110), channel_id=1, replica_groups=mesh['z'=16,'x'=4,'col'=8] {'x'}, dimensions={0} | all-to-all | bytes 1048576 | tf_op jit(solution)/shard_map/all_to_all | solution.py:329
  42.6 24.5 %all_to_all.57.in_ref = bf16[16,32,128]{2,1,0:T(8,128)(2,1)S(1)} all-to-all(bf16[16,32,128]{2,1,0:T(8,128)(2,1)S(1)} %shard_map.111), channel_id=1, replica_groups=mesh['z'=16,'x'=4,'col'=8] {'z'}, dimensions={0} | all-to-all | bytes 262144 | tf_op jit(solution)/shard_map/all_to_all | solution.py:329
  67.1 15.8 %all_to_all.58 = bf16[16,32,128]{2,1,0:T(8,128)(2,1)S(1)} all-to-all(bf16[16,32,128]{2,1,0:T(8,128)(2,1)S(1)} %shard_map.112), channel_id=1, replica_groups=mesh['z'=16,'x'=4,'col'=8] {'z'}, dimensions={0} | all-to-all | bytes 262144 | tf_op jit(solution)/shard_map/all_to_all | solution.py:329
  83.0 9.3 %all_to_all.59.v_ref = bf16[4,32,16,128]{3,2,1,0:T(8,128)(2,1)S(1)} all-to-all(bf16[4,32,16,128]{3,2,1,0:T(8,128)(2,1)S(1)} %broadcast_in_dim.6), channel_id=1, replica_groups=mesh['z'=16,'x'=4,'col'=8] {'x'}, dimensions={0} | all-to-all | bytes 1048576 | tf_op jit(solution)/shard_map/all_to_all | solution.py:329
  92.4 1.0 shard_map.113
  93.4 19.8 %all_to_all.60.l_ref = bf16[8,16,2816]{2,1,0:T(8,128)(2,1)S(1)} all-to-all(bf16[8,16,2816]{2,1,0:T(8,128)(2,1)S(1)} %shard_map.113), channel_id=1, replica_groups=mesh['z'=16,'x'=4,'col'=8] {'col'}, dimensions={0} | all-to-all | bytes 1441792 | tf_op jit(solution)/shard_map/all_to_all | solution.py:329
  113.2 1.8 shard_map.114
  115.0 0.1 convert_element_type.18
  115.1 11.0 %all_to_all.61 = f16[4,16,32,128]{3,2,1,0:T(8,128)(2,1)S(1)} all-to-all(f16[4,16,32,128]{3,2,1,0:T(8,128)(2,1)S(1)} %convert_element_type.18), channel_id=1, replica_groups=mesh['z'=16,'x'=4,'col'=8] {'x'}, dimensions={0} | all-to-all | bytes 1048576 | tf_op jit(solution)/shard_map/all_to_all | solution.py:329
  126.2 15.4 %all_to_all.62 = f16[16,32,128]{2,1,0:T(8,128)(2,1)S(1)} all-to-all(f16[16,32,128]{2,1,0:T(8,128)(2,1)S(1)} %convert_element_type.20), channel_id=1, replica_groups=mesh['z'=16,'x'=4,'col'=8] {'z'}, dimensions={0} | all-to-all | bytes 262144 | tf_op jit(solution)/shard_map/all_to_all | solution.py:329
  141.8 11.1 %all_to_all.63.q_ref = f32[8,8,128]{2,1,0:T(8,128)S(1)} all-to-all(f32[8,8,128]{2,1,0:T(8,128)S(1)} %shard_map.115), channel_id=1, replica_groups=mesh['z'=16,'x'=4,'col'=8] {'col'}, dimensions={0} | all-to-all | bytes 65536 | tf_op jit(solution)/shard_map/all_to_all | solution.py:329
  152.9 0.1 shard_map.116
  153.1 15.0 %all_to_all.64 = f16[16,32,128]{2,1,0:T(8,128)(2,1)S(1)} all-to-all(f16[16,32,128]{2,1,0:T(8,128)(2,1)S(1)} %broadcast_in_dim.7), channel_id=1, replica_groups=mesh['z'=16,'x'=4,'col'=8] {'z'}, dimensions={0} | all-to-all | bytes 262144 | tf_op jit(solution)/shard_map/all_to_all | solution.py:329
  168.2 9.3 %all_to_all.65 = f16[4,32,16,128]{3,2,1,0:T(8,128)(2,1)S(1)} all-to-all(f16[4,32,16,128]{3,2,1,0:T(8,128)(2,1)S(1)} %broadcast_in_dim.8), channel_id=1, replica_groups=mesh['z'=16,'x'=4,'col'=8] {'x'}, dimensions={0} | all-to-all | bytes 1048576 | tf_op jit(solution)/shard_map/all_to_all | solution.py:329
  177.6 1.3 shard_map.117
  (21 shorter events, 0.7 us)
Async XLA Ops:
  0.6 1.5 copy-start
  2.1 1.2 copy-start.2
  3.3 1.0 copy-start.3
  4.4 0.9 copy-start.4
  5.3 0.9 copy-start.5
  6.2 0.9 copy-start.6
  42.5 49.9 %copy-start.1 = (bf16[4,2,224,512]{3,2,1,0:T(8,128)(2,1)S(1)}, bf16[4,2,224,512]{3,2,1,0:T(8,128)(2,1)}, u32[]{:S(2)}) copy-start(bf16[4,2,224,512]{3,2,1,0:T(8,128)(2,1)} %a.7) | copy-start | bytes 5505028

commit v4 on v3

--- a/solution.py
+++ b/solution.py
@@ -7,6 +7,7 @@
 from jax.experimental.pallas import tpu as pltpu
 from jax.sharding import Mesh
 from jax.sharding import PartitionSpec as P
+
 
 F32 = jnp.float32
 BF16 = jnp.bfloat16
@@ -16,19 +17,21 @@
 LIMIT = 16 * 2**20
 WIRE = jnp.float16
 TAIL = BF16
+COL = ("y", "core")
+FIRST = 64 * 2**20 - 2**16 - 800 * 2**10
 SECOND = 8
 TOP = 2.0**15
 HBM = pl.BlockSpec(memory_space=pltpu.HBM)
 
 
-def call(kernel, outs, *args, specs=None, scratch=()):
+def call(kernel, outs, *args, specs=None, out_specs=None, scratch=(), limit=LIMIT):
     return pl.pallas_call(
         kernel,
         out_shape=outs,
         in_specs=specs or [VMEM] * len(args),
-        out_specs=jax.tree.map(lambda _: VMEM, outs),
+        out_specs=out_specs or jax.tree.map(lambda _: VMEM, outs),
         scratch_shapes=scratch,
-        compiler_params=pltpu.CompilerParams(vmem_limit_bytes=LIMIT),
+        compiler_params=pltpu.CompilerParams(vmem_limit_bytes=limit),
     )(*args)
 
 
@@ -73,6 +76,37 @@
             if part == 0
         ]
 
+        self.places = []
+        for f, w in enumerate(weights):
+            assert w.shape[0] == xs
+            for k in range(w.shape[1]) if w.ndim == 4 else (None,):
+                self.places.append((f, k, w.shape[-2]))
+        self.width = min(w.shape[-1] for w in weights)
+        self.strips = []
+        row = 0
+        for (_, _, out), (_, _, inp) in zip(self.places, self.part):
+            strips = []
+            for lane in range(0, inp, self.width):
+                strips.append((lane, min(self.width, inp - lane), row, out))
+                row += out
+            self.strips.append(strips)
+        self.packed = row
+        self.part_at = []
+        at = 0
+        for _, _, out in self.places:
+            self.part_at.append(at)
+            at += out
+        self.part_rows = at
+
+    def part_counts(self, probes):
+        lane = lax.broadcasted_iota(jnp.int32, (probes, LANES), 1)
+        outs = jnp.zeros((probes, LANES), F32) + 1.0
+        ins = outs
+        for i, (_, _, out) in enumerate(self.places):
+            outs = jnp.where(lane == i, float(out * self.rows), outs)
+            ins = jnp.where(lane == i, float(self.part[i][2] * self.cols), ins)
+        return outs, ins
+
     def counts(self, probes):
         lane = lax.broadcasted_iota(jnp.int32, (probes, LANES), 1)
         outs = jnp.zeros((probes, LANES), F32) + 1.0
@@ -109,31 +143,62 @@
     return lane_table(columns, parts[0].shape[0])
 
 
-def put_left(plan, lefts, table, out_ref):
-    dtype = out_ref.dtype
+def join_left(plan, lefts, table):
     whole = jnp.concatenate(lefts, axis=1)
     pad = plan.left_pad - plan.left_end
     if pad:
         whole = jnp.concatenate([whole, jnp.zeros((whole.shape[0], pad), F32)], axis=1)
-    whole = jnp.concatenate([whole.astype(dtype), *pieces(table, dtype)], axis=1)
-    for j in range(plan.cols):
+    return jnp.concatenate([whole, table], axis=1)
+
+
+def put_copies(plan, total, out_ref):
+    whole = total[:, : plan.left_pad].astype(BF16)
+    whole = jnp.concatenate([whole, *pieces(total[:, plan.left_pad :], BF16)], axis=1)
+    for j in range(out_ref.shape[0]):
         out_ref[j] = whole
+
+
+def pair_sum(plan, mine_ref, other_ref, out_ref):
+    put_copies(plan, mine_ref[...] + other_ref[...], out_ref)
 
 
 def dot_left(v, w):
     return lax.dot_general(v, w, (((1,), (1,)), ((), ())), preferred_element_type=F32)
 
 
-def first_left(plan, a, b, c, va, vb, vc, out_ref, *scratch):
-    held, sems = scratch[:6], scratch[6]
+def first_left(plan, a, b, c, va, vb, vc, *refs):
+    out_ref, packs = refs[0], refs[1 : 1 + plan.xs]
+    *held, sems, pack_sems = refs[1 + plan.xs :]
     copies = []
     for k, (src, dst) in enumerate(zip((va, a, vb, b, vc, c), held)):
         copies.append(pltpu.make_async_copy(src, dst, sems.at[k]))
         copies[-1].start()
+    me = lax.axis_index("x")
+    moves = []
+
+    def move(family, s):
+        part = lax.rem(me + s, plan.xs)
+        for i, (own, k, _) in enumerate(plan.places):
+            if own != family:
+                continue
+            ref = held[2 * family + 1]
+            src = ref.at[part] if k is None else ref.at[part, k]
+            for lane, lanes, row, height in plan.strips[i]:
+                moves.append(
+                    pltpu.make_async_copy(
+                        src.at[:, lane : lane + lanes],
+                        packs[s].at[row : row + height, :lanes],
+                        pack_sems.at[len(moves)],
+                    )
+                )
+                moves[-1].start()
+
     lefts, norms = [], []
     for k in range(3):
         copies[2 * k].wait()
         copies[2 * k + 1].wait()
+        for s in range(plan.xs):
+            move(k, s)
         probe, weight = held[2 * k], held[2 * k + 1]
         count = weight.shape[0] * (weight.shape[1] if weight.ndim == 4 else 1)
         for m in range(count):
@@ -141,25 +206,28 @@
             lefts.append(dot_left(matrix_of((probe,), m), w))
             wide = w.astype(F32)
             norms.append(jnp.sum(jnp.sum(wide * wide, axis=0, keepdims=True), axis=1, keepdims=True))
-    put_left(plan, lefts, lane_table(norms, lefts[0].shape[0]), out_ref)
-
-
-def vector_of(plan, v_ref, m):
-    part, first, _ = plan.where[m]
-    n = plan.ins[m] // LANES
-    return jnp.concatenate([v_ref[part, first + k] for k in range(n)], axis=1)
-
-
-def next_left(plan, a, b, c, v_ref, out_ref):
-    weights = (a, b, c)
-    probes = v_ref.shape[2]
-    lefts, squares = [], []
-    for m in range(len(plan.outs)):
-        v = vector_of(plan, v_ref, m)
+    put_copies(plan, join_left(plan, lefts, lane_table(norms, lefts[0].shape[0])), out_ref)
+    for copy in moves:
+        copy.wait()
+
+
+def next_left(plan, *refs):
+    weights, v_ref, out_ref = refs[: plan.xs], refs[-2], refs[-1]
+    vectors, squares = [], []
+    for first, n, _ in plan.part:
+        v = jnp.concatenate([v_ref[first + k] for k in range(n)], axis=1)
         wide = v.astype(F32)
         squares.append(jnp.sum(wide * wide, axis=1, keepdims=True))
-        lefts.append(dot_left(v, matrix_of(weights, m)))
-    put_left(plan, lefts, lane_table(squares, probes), out_ref)
+        vectors.append(v)
+    lefts = []
+    for weight in weights:
+        for v, strips in zip(vectors, plan.strips):
+            left = 0.0
+            for lane, lanes, row, height in strips:
+                w = weight[row : row + height, :lanes]
+                left = left + dot_left(v[:, lane : lane + lanes], w)
+            lefts.append(left)
+    out_ref[...] = join_left(plan, lefts, lane_table(squares, v_ref.shape[1]))
 
 
 def sum_of(ref):
@@ -225,13 +293,16 @@
     put_right(plan, (a, b, c), total, None, tables, out_ref, rows_ref)
 
 
-def last_right(plan, a, b, c, l_ref, v_ref, out_ref, stats_ref):
+def last_right(plan, *refs):
+    weights = refs[: plan.xs]
+    l_ref, v_ref, rows_ref, stats_ref = refs[plan.xs :]
     total, q1 = sum_left(plan, l_ref)
     probes = total.shape[0]
-    outs, ins = plan.counts(probes)
-    parts = [v_ref[x, plan.high].astype(F32) + v_ref[x, plan.low].astype(F32) for x in range(plan.xs)]
-    t1 = by_matrix(plan, parts)
-    norm = by_matrix(plan, parts, SECOND) * 1.01
+    outs, ins = plan.part_counts(probes)
+    tail = v_ref[plan.high].astype(F32) + v_ref[plan.low].astype(F32)
+    here = range(len(plan.part))
+    t1 = tail
+    norm = lane_table([tail[:, SECOND + i : SECOND + i + 1] for i in here], probes) * 1.01
     f1 = lax.rsqrt(t1 / outs + EPS)
     s1 = f1 * lax.rsqrt(f1 * f1 * q1 / ins + EPS)
     root = jnp.sqrt(q1 * 1.01 + 1e-33)
@@ -240,11 +311,34 @@
     stats_ref[0] = s1
     stats_ref[1] = scale
     stats_ref[2] = square_scale
-    squares = [
-        column * square_scale[:, m : m + 1] for m, column in enumerate(left_squares(plan, total))
-    ]
-    tables = [lane_table(of_part(plan, x, squares), probes) for x in range(plan.xs)]
-    put_right(plan, (a, b, c), total, scale, tables, None, out_ref)
+    squares = []
+    for i in here:
+        first, _, _ = plan.part[i]
+        square = 0.0
+        high, low = [], []
+        for s in range(plan.xs):
+            at = s * plan.part_rows + plan.part_at[i]
+            raw = total[:, at : at + plan.places[i][2]]
+            square = square + jnp.sum(raw * raw, axis=1, keepdims=True)
+            both = pieces(raw * scale[:, i : i + 1], BF16)
+            high.append(both[0])
+            low.append(both[1])
+        squares.append(square * square_scale[:, i : i + 1])
+        for lane, lanes, row, height in plan.strips[i]:
+            right = 0.0
+            for s in range(plan.xs):
+                w = weights[s][row : row + height, :lanes]
+                right = right + jnp.dot(high[s], w, preferred_element_type=F32)
+                right = right + jnp.dot(low[s], w, preferred_element_type=F32)
+            for k in range(lanes // LANES):
+                rows_ref[:, first + lane // LANES + k, :] = right[:, k * LANES : (k + 1) * LANES]
+    zero = jnp.zeros((probes, LANES), F32)
+    for k in range(plan.data, plan.high):
+        rows_ref[:, k, :] = zero
+    table = lane_table(squares, probes)
+    high = table.astype(TAIL).astype(F32)
+    rows_ref[:, plan.high, :] = high
+    rows_ref[:, plan.low, :] = table - high
 
 
 def split_again(plan, total, axis, dtype):
@@ -278,30 +372,32 @@
         out_ref[j] = table
 
 
-def unit(plan, y_ref, q_ref, out_ref):
+def unit(plan, stats_ref, y_ref, q_ref, out_ref):
     q = sum_of(q_ref)[:1]
+    row = lax.broadcasted_iota(jnp.int32, stats_ref.shape[1:], 0)
+    mine = row == lax.axis_index("z")
+    s1, scale, square_scale = (
+        jnp.sum(jnp.where(mine, stats_ref[k], 0.0), axis=0, keepdims=True) for k in range(3)
+    )
+    outs, _ = plan.part_counts(1)
+    t2 = (y_ref[plan.high : plan.high + 1, :] + y_ref[plan.low : plan.low + 1, :]) / square_scale
+    f2 = s1 * lax.rsqrt(s1 * s1 * t2 / outs + EPS)
+    root = jnp.sqrt(q) / scale * f2
+    table = jnp.log(jnp.maximum(root, 1e-37))
     out_ref[...] = jnp.zeros(out_ref.shape, F32)
     for i, (first, n, inp) in enumerate(plan.part):
         factor = lax.rsqrt(jnp.maximum(q[:, i : i + 1] / float(inp * plan.cols), 1e-30))
         out_ref[first : first + n, :] = y_ref[first : first + n, :] * factor
-    lane = lax.broadcasted_iota(jnp.int32, (1, LANES), 1)
-    left = y_ref[plan.high : plan.high + 1, :] + y_ref[plan.low : plan.low + 1, :]
-    left = [left[:, i : i + 1] for i in range(len(plan.part))]
-    table = jnp.where(lane < SECOND, jnp.sqrt(q), lane_table(left, 1, SECOND))
     high = table.astype(TAIL).astype(F32)
     out_ref[plan.high : plan.high + 1, :] = high
     out_ref[plan.low : plan.low + 1, :] = table - high
 
 
-def finish(plan, stats_ref, v_ref, oa, ob, oc, sa, sb, sc):
+def finish(plan, v_ref, oa, ob, oc, sa, sb, sc):
     probes = v_ref.shape[2]
     outs, ins = plan.counts(probes)
     parts = [v_ref[x, plan.high].astype(F32) + v_ref[x, plan.low].astype(F32) for x in range(plan.xs)]
-    root = by_matrix(plan, parts)
-    t2 = by_matrix(plan, parts, SECOND) / stats_ref[2]
-    s1 = stats_ref[0]
-    f2 = s1 * lax.rsqrt(s1 * s1 * t2 / outs + EPS)
-    root = root / stats_ref[1] * f2
+    root = jnp.exp(by_matrix(plan, parts))
     spread = root * lax.rsqrt(ins)
     scale = spread * lax.rsqrt(spread * spread + EPS)
     sigma = (root * lax.rsqrt(outs)).T
@@ -329,74 +425,83 @@
     return lax.all_to_all(v, axis, 0, 0, tiled=True)
 
 
-def body(gate_up, down_weight, query_output, probe_gate, probe_down, probe_query):
-    xs, zs, cols = lax.axis_size("x"), lax.axis_size("z"), lax.axis_size("col")
+def steps(gate_up, down_weight, query_output, probe_gate, probe_down, probe_query):
+    xs, zs, ys = lax.axis_size("x"), lax.axis_size("z"), lax.axis_size("y")
+    cols = lax.axis_size(COL)
     weights = (gate_up, down_weight, query_output)
     vectors = (probe_gate, probe_down, probe_query)
     probes = probe_down.shape[1]
     plan = Plan(weights, xs, zs, cols)
     bind = lambda f, *rest: functools.partial(f, *rest)
     blocks = plan.blocks
-    left_shape = sds((cols, probes, plan.left_pad + 2 * LANES), BF16)
+    left_shape = sds((probes, plan.left_pad + LANES), F32)
+    copies_shape = lambda n: sds((n, probes, plan.left_pad + 2 * LANES), BF16)
     rows = pltpu.VMEM((xs, probes, blocks, LANES), F32)
 
-    def right_shape(dtype):
-        return sds((xs, probes, blocks, LANES), dtype)
-
-    def gather(copies):
-        part = jnp.swapaxes(swap(copies, "z"), 0, 1)
-        return swap(jnp.broadcast_to(part[None], (xs, *part.shape)), "x")
+    def left_sums(left):
+        cores = lax.axis_size("core")
+        other = lax.ppermute(left, "core", [(i, (i + 1) % cores) for i in range(cores)])
+        return call(bind(pair_sum, plan), copies_shape(ys), left, other)
+
+    def by_block(copies):
+        return jnp.swapaxes(swap(copies, "z"), 0, 1)
 
     held = [pltpu.VMEM(x.shape, x.dtype) for pair in zip(vectors, weights) for x in pair]
-    left = call(
+    strips = xs * sum(len(strips) for strips in plan.strips)
+    left, *packs = call(
         bind(first_left, plan),
-        left_shape,
+        (copies_shape(cols),) + (sds((plan.packed, plan.width), BF16),) * xs,
         *weights,
         *vectors,
         specs=[HBM] * 6,
-        scratch=[*held, pltpu.SemaphoreType.DMA((6,))],
+        out_specs=(VMEM,) + (HBM,) * xs,
+        scratch=[*held, pltpu.SemaphoreType.DMA((6,)), pltpu.SemaphoreType.DMA((strips,))],
+        limit=FIRST,
     )
-    left = swap(left, "col")
-    right = call(bind(first_right, plan), right_shape(BF16), *weights, left, scratch=[rows])
+    left = swap(left, COL)
+    for s in range(1, xs):
+        packs[s] = lax.ppermute(packs[s], "x", [(i, (i + s) % xs) for i in range(xs)])
+    shape = sds((xs, probes, blocks, LANES), BF16)
+    right = call(bind(first_right, plan), shape, *weights, left, scratch=[rows])
     right = swap(right, "x")
     right = call(bind(sum_parts, plan), sds((probes, blocks, LANES), BF16), right)
     right = swap(right, "z")
-    v1 = gather(call(bind(sum_copies, plan), sds((zs, blocks, LANES), BF16), right))
-
-    left = call(bind(next_left, plan), left_shape, *weights, v1)
-    left = swap(left, "col")
-    shapes = (right_shape(F32), sds((3, probes, LANES), F32))
-    right, stats = call(bind(last_right, plan), shapes, *weights, left, v1)
-    right = swap(right.astype(WIRE), "x")
-    right = jnp.sum(right.astype(F32), axis=0).astype(WIRE)
-    right = jnp.sum(swap(right, "z").astype(F32), axis=0)
+    right = call(bind(sum_copies, plan), sds((zs, blocks, LANES), BF16), right)
+    v1 = by_block(right)
+
+    left = call(bind(next_left, plan), left_shape, *packs, v1)
+    left = swap(left_sums(left), "y")
+    shapes = (sds((probes, blocks, LANES), F32), sds((3, probes, LANES), F32))
+    right, stats = call(bind(last_right, plan), shapes, *packs, left, v1)
+    right = jnp.sum(swap(right.astype(WIRE), "z").astype(F32), axis=0)
     q2 = call(bind(own_squares, plan), sds((cols, 8, LANES), F32), right)
-    q2 = swap(q2, "col")
-    own = call(bind(unit, plan), sds((blocks, LANES), F32), right, q2)
-    v2 = gather(jnp.broadcast_to(own.astype(WIRE)[None], (zs, *own.shape))).astype(F32)
+    q2 = swap(q2, COL)
+    own = call(bind(unit, plan), sds((blocks, LANES), F32), stats, right, q2)
+    part = by_block(jnp.broadcast_to(own.astype(WIRE)[None], (zs, *own.shape)))
+    v2 = swap(jnp.broadcast_to(part[None], (xs, *part.shape)), "x").astype(F32)
     outs = tuple(sds(v.shape, F32) for v in vectors)
     outs += tuple(sds(v.shape[:-1], F32) for v in vectors)
-    return call(bind(finish, plan), outs, stats, v2)
+    return call(bind(finish, plan), outs, v2)
 
 
 def solution(mesh):
-    z = 16
-    finer = Mesh(mesh.devices.reshape(z, -1, mesh.shape["col"]), ("z", "x", "col"))
+    cols = mesh.shape["col"]
+    finer = Mesh(mesh.devices.reshape(16, -1, cols // 2, 2), ("z", "x", *COL))
     row = ("z", "x")
     in_specs = (
-        P(None, None, row, "col"),
-        P(None, row, "col"),
-        P(None, None, row, "col"),
-        P(None, None, None, "col"),
-        P(None, None, "col"),
-        P(None, None, None, "col"),
+        P(None, None, row, COL),
+        P(None, row, COL),
+        P(None, None, row, COL),
+        P(None, None, None, COL),
+        P(None, None, COL),
+        P(None, None, None, COL),
     )
     out_specs = (
-        P(None, None, None, "col"),
-        P(None, None, "col"),
-        P(None, None, None, "col"),
+        P(None, None, None, COL),
+        P(None, None, COL),
+        P(None, None, None, COL),
         P(),
         P(),
         P(),
     )
-    return jax.shard_map(body, mesh=finer, in_specs=in_specs, out_specs=out_specs, check_vma=False)
+    return jax.shard_map(steps, mesh=finer, in_specs=in_specs, out_specs=out_specs, check_vma=False)

time: 182 us -> 179 us (0.984)
  the two profiles are of different devices: /device:TPU:1 before, /device:TPU:32 now
where the time goes in v4:
time: 179 us
  blocking collectives  125 us (70%)
  starting transfers between devices  26.3 us (15%)
  waiting for transfers between devices  13.8 us (8%)
  Pallas kernels  10.5 us (6%)
    all_to_all x8, blocking collectives, swap(): return lax.all_to_all(v, axis, 0, 0, tiled=True)  125 us
    all_to_all x1, starting transfers between devices, swap(): return lax.all_to_all(v, axis, 0, 0, tiled=True)  15.2 us
    pallas_call x10, Pallas kernels, call(): pl.pallas_call(kernel, out_shape=outs, in_specs=specs or [VMEM] * len(arg...  10.5 us
    ppermute x3, starting transfers between devices, steps(): lax.ppermute(packs[s], 'x', [(i, (i + s) % xs) for i in range(xs)])  9.16 us
    ppermute x3, waiting for transfers between devices, steps(): lax.ppermute(packs[s], 'x', [(i, (i + s) % xs) for i in range(xs)])  9.14 us
  transfers between devices with their start and end apart: 5, of which 4 were waited for; matrix products, arithmetic and copies ran while one was open for 0% of the time, Pallas kernels for 0%

profile of v4, /device:TPU:32, one launch (start us, length us, event | category | flops | bytes accessed | tf_op | source)
XLA Modules:
  0.0 178.8 jit_solution(8626296541858239752)
XLA Ops:
  0.6 4.8 %shard_map.109 = (bf16[8,16,2816]{2,1,0:T(8,128)(2,1)}, bf16[832,512]{1,0:T(8,128)(2,1)}, bf16[832,512]{1,0:T(8,128)(2,1)}, bf16[832,512]{1,0:T(8,128)(2,1)}, bf16[832,512]{1,0:T(8,128)(2,1)}) custom-call(bf16[4,2,224,512]{3,2,1,0:T(8,128)(2,1)} %a.3, bf16[4,64,1792]{2,1,0:T(8,128)(2,1)} %b.3, bf16[4,2,64,512]{3,2,1,0:T(8,128)(2,1)} %c.3, ...), custom_call_target="tpu_custom_call" | custom-call | tf_op jit(solution)/shard_map/pallas_call | solution.py:28
  5.4 17.1 %all_to_all.45.l_ref = bf16[8,16,2816]{2,1,0:T(8,128)(2,1)S(1)} all-to-all(bf16[8,16,2816]{2,1,0:T(8,128)(2,1)} %get-tuple-element.17), channel_id=1, replica_groups=mesh['z'=16,'x'=4,'y'=4,'core'=2] {'y','core'}, dimensions={0} | all-to-all | bytes 1441792 | tf_op jit(solution)/shard_map/all_to_all | solution.py:425
  22.5 1.5 copy-done
  24.0 1.3 shard_map.110
  25.3 13.4 %all_to_all.46.in_ref = bf16[4,16,32,128]{3,2,1,0:T(8,128)(2,1)S(1)} all-to-all(bf16[4,16,32,128]{3,2,1,0:T(8,128)(2,1)S(1)} %shard_map.110), channel_id=1, replica_groups=mesh['z'=16,'x'=4,'y'=4,'core'=2] {'x'}, dimensions={0} | all-to-all | bytes 1048576 | tf_op jit(solution)/shard_map/all_to_all | solution.py:425
  38.7 0.7 shard_map.111
  39.5 15.2 %all-to-all-start.2 = ((bf16[16,32,128]{2,1,0:T(8,128)(2,1)}), bf16[16,32,128]{2,1,0:T(8,128)(2,1)S(1)}, u32[]{:S(2)}, u32[]{:S(2)}) async-start(bf16[16,32,128]{2,1,0:T(8,128)(2,1)} %shard_map.111), calls=%async_computation.2 | async-start | bytes 262144 | tf_op jit(solution)/shard_map/all_to_all | solution.py:425
  54.7 2.5 %collective-permute-start = (bf16[832,512]{1,0:T(8,128)(2,1)}, bf16[832,512]{1,0:T(8,128)(2,1)S(1)}, u32[]{:S(2)}, u32[]{:S(2)}) collective-permute-start(bf16[832,512]{1,0:T(8,128)(2,1)} %get-tuple-element.14), channel_id=1, source_target_pairs={{0,8},{8,16},{16,24},{24,0},{1,9},{9,17},{17,25},{25,1},{2,10},{10... | collective-permute-start | bytes 2555912 | tf_op jit(solution)/shard_map/ppermute | solution.py:463
  57.2 4.0 %collective-permute-start.1 = (bf16[832,512]{1,0:T(8,128)(2,1)}, bf16[832,512]{1,0:T(8,128)(2,1)S(1)}, u32[]{:S(2)}, u32[]{:S(2)}) collective-permute-start(bf16[832,512]{1,0:T(8,128)(2,1)} %get-tuple-element.15), channel_id=1, source_target_pairs={{0,16},{8,24},{16,0},{24,8},{1,17},{9,25},{17,1},{25,9},{2,18},{10... | collective-permute-start | bytes 2555912 | tf_op jit(solution)/shard_map/ppermute | solution.py:463
  61.1 2.7 %collective-permute-start.2 = (bf16[832,512]{1,0:T(8,128)(2,1)}, bf16[832,512]{1,0:T(8,128)(2,1)S(1)}, u32[]{:S(2)}, u32[]{:S(2)}) collective-permute-start(bf16[832,512]{1,0:T(8,128)(2,1)} %get-tuple-element.16), channel_id=1, source_target_pairs={{0,24},{8,0},{16,8},{24,16},{1,25},{9,1},{17,9},{25,17},{2,26},{10... | collective-permute-start | bytes 2555912 | tf_op jit(solution)/shard_map/ppermute | solution.py:463
  63.9 3.3 %all-to-all-done.2.in_ref = bf16[16,32,128]{2,1,0:T(8,128)(2,1)S(1)} async-done(((bf16[16,32,128]{2,1,0:T(8,128)(2,1)}), bf16[16,32,128]{2,1,0:T(8,128)(2,1)S(1)}, u32[]{:S(2)}, u32[]{:S(2)}) %all-to-all-start.2) | async-done | bytes 131104 | tf_op jit(solution)/shard_map/all_to_all | solution.py:425
  67.3 21.1 %all_to_all.47 = bf16[16,32,128]{2,1,0:T(8,128)(2,1)S(1)} all-to-all(bf16[16,32,128]{2,1,0:T(8,128)(2,1)S(1)} %shard_map.112), channel_id=1, replica_groups=mesh['z'=16,'x'=4,'y'=4,'core'=2] {'z'}, dimensions={0} | all-to-all | bytes 262144 | tf_op jit(solution)/shard_map/all_to_all | solution.py:425
  88.4 6.6 %collective-permute-done.refs_1_ = bf16[832,512]{1,0:T(8,128)(2,1)S(1)} collective-permute-done((bf16[832,512]{1,0:T(8,128)(2,1)}, bf16[832,512]{1,0:T(8,128)(2,1)S(1)}, u32[]{:S(2)}, u32[]{:S(2)}) %collective-permute-start) | collective-permute-done | bytes 852000 | tf_op jit(solution)/shard_map/ppermute | solution.py:463
  95.0 2.5 %collective-permute-done.2.refs_3_ = bf16[832,512]{1,0:T(8,128)(2,1)S(1)} collective-permute-done((bf16[832,512]{1,0:T(8,128)(2,1)}, bf16[832,512]{1,0:T(8,128)(2,1)S(1)}, u32[]{:S(2)}, u32[]{:S(2)}) %collective-permute-start.2) | collective-permute-done | bytes 852000 | tf_op jit(solution)/shard_map/ppermute | solution.py:463
  97.5 1.0 shard_map.113.mine_ref
  98.5 2.0 %collective-permute-start.3 = (f32[16,2688]{1,0:T(8,128)S(1)}, f32[16,2688]{1,0:T(8,128)S(1)}, u32[]{:S(2)}, u32[]{:S(2)}) collective-permute-start(f32[16,2688]{1,0:T(8,128)S(1)} %shard_map.113.mine_ref), channel_id=1, source_target_pairs={{0,1},{1,0},{2,3},{3,2},{4,5},{5,4},{6,7},{7,6},{8,9},{9,8},{10,11... | collective-permute-start | bytes 516104 | tf_op jit(solution)/shard_map/ppermute | solution.py:443
  100.5 1.4 collective-permute-done.3.other_ref
  101.9 10.7 %all_to_all.48.refs_4_ = bf16[4,16,2816]{2,1,0:T(8,128)(2,1)S(1)} all-to-all(bf16[4,16,2816]{2,1,0:T(8,128)(2,1)S(1)} %shard_map.114), channel_id=1, replica_groups=mesh['z'=16,'x'=4,'y'=4,'core'=2] {'y'}, dimensions={0} | all-to-all | bytes 720896 | tf_op jit(solution)/shard_map/all_to_all | solution.py:425
  112.6 1.2 shard_map.115
  113.8 25.3 %all_to_all.49 = f16[16,32,128]{2,1,0:T(8,128)(2,1)S(1)} all-to-all(f16[16,32,128]{2,1,0:T(8,128)(2,1)S(1)} %convert_element_type.12), channel_id=1, replica_groups=mesh['z'=16,'x'=4,'y'=4,'core'=2] {'z'}, dimensions={0} | all-to-all | bytes 262144 | tf_op jit(solution)/shard_map/all_to_all | solution.py:425
  139.3 7.8 %all_to_all.50.q_ref = f32[8,8,128]{2,1,0:T(8,128)S(1)} all-to-all(f32[8,8,128]{2,1,0:T(8,128)S(1)} %shard_map.116), channel_id=1, replica_groups=mesh['z'=16,'x'=4,'y'=4,'core'=2] {'y','core'}, dimensions={0} | all-to-all | bytes 65536 | tf_op jit(solution)/shard_map/all_to_all | solution.py:425
  147.3 18.3 %all_to_all.51 = f16[16,32,128]{2,1,0:T(8,128)(2,1)S(1)} all-to-all(f16[16,32,128]{2,1,0:T(8,128)(2,1)S(1)} %broadcast_in_dim.4), channel_id=1, replica_groups=mesh['z'=16,'x'=4,'y'=4,'core'=2] {'z'}, dimensions={0} | all-to-all | bytes 262144 | tf_op jit(solution)/shard_map/all_to_all | solution.py:425
  165.8 11.8 %all_to_all.52 = f16[4,32,16,128]{3,2,1,0:T(8,128)(2,1)S(1)} all-to-all(f16[4,32,16,128]{3,2,1,0:T(8,128)(2,1)S(1)} %broadcast_in_dim.5), channel_id=1, replica_groups=mesh['z'=16,'x'=4,'y'=4,'core'=2] {'x'}, dimensions={0} | all-to-all | bytes 1048576 | tf_op jit(solution)/shard_map/all_to_all | solution.py:425
  177.6 1.2 shard_map.118
  (20 shorter events, 0.6 us)
Async XLA Ops:
  0.6 21.9 %copy-start.3 = (bf16[4,2,64,512]{3,2,1,0:T(8,128)(2,1)S(1)}, bf16[4,2,64,512]{3,2,1,0:T(8,128)(2,1)}, u32[]{:S(2)}) copy-start(bf16[4,2,64,512]{3,2,1,0:T(8,128)(2,1)} %c.3) | copy-start | bytes 1572868
  5.4 17.1 %copy-start.1 = (bf16[4,64,1792]{2,1,0:T(8,128)(2,1)S(1)}, bf16[4,64,1792]{2,1,0:T(8,128)(2,1)}, u32[]{:S(2)}) copy-start(bf16[4,64,1792]{2,1,0:T(8,128)(2,1)} %b.3) | copy-start | bytes 2752516
  22.5 1.5 copy-start
  25.3 72.2 %copy-start.2 = (bf16[832,512]{1,0:T(8,128)(2,1)S(1)}, bf16[832,512]{1,0:T(8,128)(2,1)}, u32[]{:S(2)}) copy-start(bf16[832,512]{1,0:T(8,128)(2,1)} %get-tuple-element.13.refs_0_) | copy-start | bytes 2555908
  39.5 27.7 %all-to-all-start.2 = ((bf16[16,32,128]{2,1,0:T(8,128)(2,1)}), bf16[16,32,128]{2,1,0:T(8,128)(2,1)S(1)}, u32[]{:S(2)}, u32[]{:S(2)}) async-start(bf16[16,32,128]{2,1,0:T(8,128)(2,1)} %shard_map.111), calls=%async_computation.2 | async-start | bytes 262144 | tf_op jit(solution)/shard_map/all_to_all | solution.py:425
  54.7 40.3 %collective-permute-start = (bf16[832,512]{1,0:T(8,128)(2,1)}, bf16[832,512]{1,0:T(8,128)(2,1)S(1)}, u32[]{:S(2)}, u32[]{:S(2)}) collective-permute-start(bf16[832,512]{1,0:T(8,128)(2,1)} %get-tuple-element.14), channel_id=1, source_target_pairs={{0,8},{8,16},{16,24},{24,0},{1,9},{9,17},{17,25},{25,1},{2,10},{10... | collective-permute-start | bytes 2555912 | tf_op jit(solution)/shard_map/ppermute | solution.py:463
  57.2 37.8 %collective-permute-start.1 = (bf16[832,512]{1,0:T(8,128)(2,1)}, bf16[832,512]{1,0:T(8,128)(2,1)S(1)}, u32[]{:S(2)}, u32[]{:S(2)}) collective-permute-start(bf16[832,512]{1,0:T(8,128)(2,1)} %get-tuple-element.15), channel_id=1, source_target_pairs={{0,16},{8,24},{16,0},{24,8},{1,17},{9,25},{17,1},{25,9},{2,18},{10... | collective-permute-start | bytes 2555912 | tf_op jit(solution)/shard_map/ppermute | solution.py:463
  61.1 36.4 %collective-permute-start.2 = (bf16[832,512]{1,0:T(8,128)(2,1)}, bf16[832,512]{1,0:T(8,128)(2,1)S(1)}, u32[]{:S(2)}, u32[]{:S(2)}) collective-permute-start(bf16[832,512]{1,0:T(8,128)(2,1)} %get-tuple-element.16), channel_id=1, source_target_pairs={{0,24},{8,0},{16,8},{24,16},{1,25},{9,1},{17,9},{25,17},{2,26},{10... | collective-permute-start | bytes 2555912 | tf_op jit(solution)/shard_map/ppermute | solution.py:463
  98.5 3.3 %collective-permute-start.3 = (f32[16,2688]{1,0:T(8,128)S(1)}, f32[16,2688]{1,0:T(8,128)S(1)}, u32[]{:S(2)}, u32[]{:S(2)}) collective-permute-start(f32[16,2688]{1,0:T(8,128)S(1)} %shard_map.113.mine_ref), channel_id=1, source_target_pairs={{0,1},{1,0},{2,3},{3,2},{4,5},{5,4},{6,7},{7,6},{8,9},{9,8},{10,11... | collective-permute-start | bytes 516104 | tf_op jit(solution)/shard_map/ppermute | solution.py:443
